TPU v7x, 32 devices: a whole 2x2x4 slice. The times are simulated.
32 devices in a mesh: rows: 8 (over z, x), head: 4 (over y, core).
Axes of the slice: x: 2, y: 2, z: 4, core: 2. Of those that a mesh axis runs over, the one named last changes fastest.
Arguments:
- inputs: bfloat16 [2, 32, 512, 768], P(None, ('rows', 'head')), may hold values from -6 to 6
- qkv_weight: bfloat16 [768, 2304], P('rows', 'head'), may hold values from -0.3125 to 0.3125
- out_weight: bfloat16 [768, 768], P('rows', 'head'), may hold values from -0.625 to 0.625
- up_weight: bfloat16 [768, 3072], P('rows', 'head'), may hold values from -0.21875 to 0.21875
- down_weight: bfloat16 [3072, 768], P('rows', 'head'), may hold values from -0.109375 to 0.109375
- biases: bfloat16 [8, 768], P('head', 'rows'), may hold values from -1.1953125 to 1.1953125
- norm_params: bfloat16 [4, 768], P('head', 'rows'), may hold values from -0.6 to 1.65
- cotangent: bfloat16 [2, 32, 512, 768], P(None, ('rows', 'head')), may hold values from -6 to 6
- boundaries: int32 [2, 32], P(None, 'rows'), may hold values from 1 to 511, as said below
- lengths: int32 [2, 32], P(None, 'rows'), may hold values from 257 to 512, as said below
Outputs:
- output: bfloat16 [2, 32, 512, 768], P(None, ('rows', 'head'))
- input_grad: float32 [2, 32, 512, 768], P(None, ('rows', 'head'))
- qkv_grad: float32 [768, 2304], P('rows', 'head')
- out_grad: float32 [768, 768], P('rows', 'head')
- up_grad: float32 [768, 3072], P('rows', 'head')
- down_grad: float32 [3072, 768], P('rows', 'head')
- bias_grad: float32 [8, 768], P('head', 'rows')
- norm_grad: float32 [4, 768], P('head', 'rows')
Inputs may be any that keep to these rules, and one draw needn't show every extreme that they name: `boundaries`: each row's boundary lies below its own length, so both sentences of a row hold tokens. `lengths`: every length exceeds half of 512.
All inputs are finite; a program needn't handle non-finite values.
Results may differ from a plain program's by a relative error of at most 0.017.
The roundings to bfloat16 on the way count: a program that leaves them out, or rounds other values in their place, can miss the bound.
Values may be sent and summed in bfloat16 or wider, within the bound.
A program may use at most 192 MiB of HBM per device.

v0:
```python
import jax
import jax.numpy as jnp
from jax import lax
from jax.sharding import PartitionSpec as P

D = 768
HEADS = 12
HD = 64
FF = 3072
SEQ = 512


EPSILON = 1e-06
ROOT_HALF = 0.7071067811865476
INVERSE_ROOT_TWO_PI = 0.3989422804014327


def contract_rows(left, right):
    return lax.dot_general(
        left, right, (((0,), (0,)), ((), ())), preferred_element_type=jnp.float32
    )


def contract_cols(left, right):
    return lax.dot_general(
        left, right, (((1,), (1,)), ((), ())), preferred_element_type=jnp.float32
    )


def norm_forward(values_in, gain_row, shift_row):
    average = jnp.mean(values_in, axis=-1, keepdims=True)
    centered = values_in - average
    variance = jnp.mean(centered * centered, axis=-1, keepdims=True)
    inverse_scale = lax.rsqrt(variance + EPSILON)
    normed = centered * inverse_scale
    return (normed * gain_row + shift_row, normed, inverse_scale)


def norm_backward(grad_out, normed, inverse_scale, gain_row):
    grad_normed = grad_out * gain_row
    first_mean = jnp.mean(grad_normed, axis=-1, keepdims=True)
    second_mean = jnp.mean(grad_normed * normed, axis=-1, keepdims=True)
    grad_in = inverse_scale * (grad_normed - first_mean - normed * second_mean)
    return (grad_in, jnp.sum(grad_out * normed, axis=0), jnp.sum(grad_out, axis=0))


def masked_scores(queries, keys_in, bound, length):
    positions = lax.broadcasted_iota(jnp.int32, (SEQ,), 0)
    segment = positions >= bound
    allowed = (segment[:, None] == segment[None, :]) & (positions[None, :] < length)
    scores = jnp.einsum(
        "qhe,khe->hqk", queries, keys_in, preferred_element_type=jnp.float32
    ) * HD ** (-0.5)
    return jnp.where(allowed[None], scores, -1e30)


def attend_forward(pieces):
    queries, keys_in, values_in, bound, length = pieces
    scores = masked_scores(queries, keys_in, bound, length)
    highest = jnp.max(scores, axis=-1, keepdims=True)
    raised = jnp.exp(scores - highest)
    totals = jnp.sum(raised, axis=-1, keepdims=True)
    weights_low = (raised / totals).astype(jnp.bfloat16)
    context = jnp.einsum("hqk,khe->qhe", weights_low, values_in, preferred_element_type=jnp.float32)
    log_total = (highest + jnp.log(totals))[..., 0]
    return (context.astype(jnp.bfloat16), log_total)


def attend_backward(pieces):
    queries, keys_in, values_in, bound, length, log_total, grad_context = pieces
    scores = masked_scores(queries, keys_in, bound, length)
    weights_full = jnp.exp(scores - log_total[..., None])
    weights_low = weights_full.astype(jnp.bfloat16)
    grad_values = jnp.einsum(
        "hqk,qhe->khe", weights_low, grad_context, preferred_element_type=jnp.float32
    )
    grad_weights = jnp.einsum(
        "qhe,khe->hqk", grad_context, values_in, preferred_element_type=jnp.float32
    )
    inner_sum = jnp.sum(weights_full * grad_weights, axis=-1, keepdims=True)
    grad_scores = (weights_full * (grad_weights - inner_sum)).astype(jnp.bfloat16)
    grad_queries = jnp.einsum(
        "hqk,khe->qhe", grad_scores, keys_in, preferred_element_type=jnp.float32
    ) * HD ** (-0.5)
    grad_keys = jnp.einsum(
        "hqk,qhe->khe", grad_scores, queries, preferred_element_type=jnp.float32
    ) * HD ** (-0.5)
    return jnp.stack([grad_queries, grad_keys, grad_values], axis=2).astype(jnp.bfloat16)


def split_heads(project, bounds, lengths_here, groups):
    seq_per = project.shape[0] // SEQ
    heads_dev = HEADS // groups
    spread = project.reshape(seq_per, SEQ, groups, 3 * D // groups)
    items = lax.all_to_all(spread, "head", split_axis=2, concat_axis=0, tiled=True)
    return (items.reshape(-1, SEQ, heads_dev, 3, HD), bounds, lengths_here)


def merge_heads(context_items, seq_per):
    width = context_items.shape[2] * HD
    joined = lax.all_to_all(
        context_items.reshape(-1, SEQ, 1, width), "head", split_axis=0, concat_axis=2, tiled=True
    )
    return joined.reshape(seq_per * SEQ, D)


def grad_to_items(grad_context, seq_per, groups):
    heads_dev = HEADS // groups
    spread = grad_context.reshape(seq_per, SEQ, groups, D // groups)
    items = lax.all_to_all(spread, "head", split_axis=2, concat_axis=0, tiled=True)
    return items.reshape(-1, SEQ, heads_dev, HD)


def grad_to_tokens(grad_items, seq_per):
    width = grad_items.shape[2] * 3 * HD
    joined = lax.all_to_all(
        grad_items.reshape(-1, SEQ, 1, width), "head", split_axis=0, concat_axis=2, tiled=True
    )
    return joined.reshape(seq_per * SEQ, 3 * D)


def gather_weights(qkv_weight, out_weight, up_weight, down_weight, biases, norm_params):
    by_head = (
        lax.all_gather(qkv_weight, "head", axis=1, tiled=True),
        lax.all_gather(out_weight, "head", axis=1, tiled=True),
        lax.all_gather(up_weight, "head", axis=1, tiled=True),
        lax.all_gather(down_weight, "head", axis=1, tiled=True),
        lax.all_gather(biases, "head", axis=0, tiled=True),
        lax.all_gather(norm_params, "head", axis=0, tiled=True),
    )
    return (
        lax.all_gather(by_head[0], "rows", axis=0, tiled=True),
        lax.all_gather(by_head[1], "rows", axis=0, tiled=True),
        lax.all_gather(by_head[2], "rows", axis=0, tiled=True),
        lax.all_gather(by_head[3], "rows", axis=0, tiled=True),
        lax.all_gather(by_head[4], "rows", axis=1, tiled=True),
        lax.all_gather(by_head[5], "rows", axis=1, tiled=True),
    )


def reduce_grads(running):
    rows_done = (
        lax.psum_scatter(running[0], "rows", scatter_dimension=0, tiled=True),
        lax.psum_scatter(running[1], "rows", scatter_dimension=0, tiled=True),
        lax.psum_scatter(running[2], "rows", scatter_dimension=0, tiled=True),
        lax.psum_scatter(running[3], "rows", scatter_dimension=0, tiled=True),
        lax.psum_scatter(running[4], "rows", scatter_dimension=1, tiled=True),
        lax.psum_scatter(running[5], "rows", scatter_dimension=1, tiled=True),
    )
    return (
        lax.psum_scatter(
            rows_done[0].astype(jnp.bfloat16), "head", scatter_dimension=1, tiled=True
        ).astype(jnp.float32),
        lax.psum_scatter(
            rows_done[1].astype(jnp.bfloat16), "head", scatter_dimension=1, tiled=True
        ).astype(jnp.float32),
        lax.psum_scatter(
            rows_done[2].astype(jnp.bfloat16), "head", scatter_dimension=1, tiled=True
        ).astype(jnp.float32),
        lax.psum_scatter(
            rows_done[3].astype(jnp.bfloat16), "head", scatter_dimension=1, tiled=True
        ).astype(jnp.float32),
        lax.psum_scatter(
            rows_done[4].astype(jnp.bfloat16), "head", scatter_dimension=0, tiled=True
        ).astype(jnp.float32),
        lax.psum_scatter(
            rows_done[5].astype(jnp.bfloat16), "head", scatter_dimension=0, tiled=True
        ).astype(jnp.float32),
    )


def layer_step(params, block_in, block_cot, bounds, lengths_here):
    qkv_full, out_full, up_full, down_full, bias_full, norm_full = params
    seq_per = block_in.shape[0]
    groups = lax.axis_size("head")
    tokens = block_in.reshape(seq_per * SEQ, D)
    bias_float = bias_full.astype(jnp.float32)
    norm_float = norm_full.astype(jnp.float32)
    zero_part = jnp.zeros((HEADS, HD), jnp.float32)
    head_bias = jnp.stack(
        [bias_float[0].reshape(HEADS, HD), zero_part, bias_float[1].reshape(HEADS, HD)], axis=1
    ).reshape(3 * D)
    project = (jnp.dot(tokens, qkv_full, preferred_element_type=jnp.float32) + head_bias).astype(
        jnp.bfloat16
    )
    items, item_bounds, item_lengths = split_heads(project, bounds, lengths_here, groups)
    queries = items[:, :, :, 0]
    keys_all = items[:, :, :, 1]
    values_all = items[:, :, :, 2]
    context_items, log_total = lax.map(
        attend_forward, (queries, keys_all, values_all, item_bounds, item_lengths)
    )
    context_tok = merge_heads(context_items, seq_per)
    attended = jnp.dot(context_tok, out_full, preferred_element_type=jnp.float32) + bias_float[2]
    hidden, normed_one, scale_one = norm_forward(
        tokens.astype(jnp.float32) + attended, norm_float[0], norm_float[1]
    )
    hidden_low = hidden.astype(jnp.bfloat16)
    inner_pre = jnp.dot(hidden_low, up_full, preferred_element_type=jnp.float32) + bias_float[
        4:8
    ].reshape(FF)
    active_low = jax.nn.gelu(inner_pre, approximate=False).astype(jnp.bfloat16)
    outer_out = jnp.dot(active_low, down_full, preferred_element_type=jnp.float32) + bias_float[3]
    output_float, normed_two, scale_two = norm_forward(
        hidden + outer_out, norm_float[2], norm_float[3]
    )
    output_block = output_float.astype(jnp.bfloat16).reshape(seq_per, SEQ, D)
    grad_out = block_cot.reshape(seq_per * SEQ, D).astype(jnp.float32)
    grad_two, gain_two, shift_two = norm_backward(grad_out, normed_two, scale_two, norm_float[2])
    grad_two_low = grad_two.astype(jnp.bfloat16)
    down_grad = contract_rows(active_low, grad_two_low)
    grad_active = contract_cols(grad_two_low, down_full)
    slope = (
        0.5 * (1.0 + lax.erf(inner_pre * ROOT_HALF))
        + inner_pre * jnp.exp(-0.5 * inner_pre * inner_pre) * INVERSE_ROOT_TWO_PI
    )
    grad_inner = grad_active * slope
    grad_inner_low = grad_inner.astype(jnp.bfloat16)
    up_grad = contract_rows(hidden_low, grad_inner_low)
    grad_hidden = contract_cols(grad_inner_low, up_full) + grad_two
    grad_one, gain_one, shift_one = norm_backward(grad_hidden, normed_one, scale_one, norm_float[0])
    grad_one_low = grad_one.astype(jnp.bfloat16)
    out_grad = contract_rows(context_tok, grad_one_low)
    grad_context = contract_cols(grad_one_low, out_full).astype(jnp.bfloat16)
    grad_items = grad_to_items(grad_context, seq_per, groups)
    grad_project_items = lax.map(
        attend_backward,
        (queries, keys_all, values_all, item_bounds, item_lengths, log_total, grad_items),
    )
    grad_project = grad_to_tokens(grad_project_items, seq_per)
    qkv_grad = contract_rows(tokens, grad_project)
    grad_input = contract_cols(grad_project, qkv_full) + grad_one
    project_sums = jnp.sum(grad_project, axis=0, dtype=jnp.float32).reshape(HEADS, 3, HD)
    bias_grad = jnp.concatenate(
        [
            project_sums[:, 0].reshape(1, D),
            project_sums[:, 2].reshape(1, D),
            jnp.sum(grad_one, axis=0).reshape(1, D),
            jnp.sum(grad_two, axis=0).reshape(1, D),
            jnp.sum(grad_inner, axis=0).reshape(4, D),
        ],
        axis=0,
    )
    norm_grad = jnp.stack([gain_one, shift_one, gain_two, shift_two])
    return (
        output_block,
        grad_input.reshape(seq_per, SEQ, D),
        (qkv_grad, out_grad, up_grad, down_grad, bias_grad, norm_grad),
    )


def shards(
    inputs,
    qkv_weight,
    out_weight,
    up_weight,
    down_weight,
    biases,
    norm_params,
    cotangent,
    boundaries,
    lengths,
):
    outputs_all = []
    inputs_grads = []
    running = None
    for micro_index in range(inputs.shape[0]):
        params = gather_weights(qkv_weight, out_weight, up_weight, down_weight, biases, norm_params)
        output_block, grad_block, grads_now = layer_step(
            params,
            inputs[micro_index],
            cotangent[micro_index],
            boundaries[micro_index],
            lengths[micro_index],
        )
        outputs_all.append(output_block)
        inputs_grads.append(grad_block)
        if micro_index == 0:
            running = grads_now
        else:
            running = tuple((sum_now + add_now for sum_now, add_now in zip(running, grads_now)))
    final = reduce_grads(running)
    return (
        jnp.stack(outputs_all),
        jnp.stack(inputs_grads),
        final[0],
        final[1],
        final[2],
        final[3],
        final[4],
        final[5],
    )


def solution(mesh):
    placed = (
        P(None, ("rows", "head"), None, None),
        P("rows", "head"),
        P("rows", "head"),
        P("rows", "head"),
        P("rows", "head"),
        P("head", "rows"),
        P("head", "rows"),
        P(None, ("rows", "head"), None, None),
        P(None, "rows"),
        P(None, "rows"),
    )
    return jax.shard_map(
        shards,
        mesh=mesh,
        in_specs=placed,
        out_specs=(
            P(None, ("rows", "head"), None, None),
            P(None, ("rows", "head"), None, None),
            P("rows", "head"),
            P("rows", "head"),
            P("rows", "head"),
            P("rows", "head"),
            P("head", "rows"),
            P("head", "rows"),
        ),
        check_vma=False,
    )
```

profile of v0, /device:TPU:0, one launch (start us, length us, event | category | flops | bytes accessed | tf_op | source)
XLA Modules:
  0.0 1183.9 jit_solution(4016477285375403573)
XLA Ops:
  7.2 8.8 all-gather
  18.5 5.6 all_gather.52
  25.0 8.1 all_gather.56
  33.1 5.1 all-gather.1
  38.1 27.4 %all-gather.2 = bf16[8,96,8]{1,2,0:T(8,128)(2,1)S(1)} all-gather(bf16[1,96,8]{1,2,0:T(8,128)(2,1)S(1)} %bitcast.451), channel_id=1, replica_groups=mesh['rows'=8,'head'=4] {'rows'}, dimensions={0}, use_global_device_ids=true | all-gather | bytes 13824 | tf_op jit(solution)/shard_map/all_gather | solution.py:136
  66.6 16.7 %all-gather.10.cloned.1.call-done = bf16[768,2304]{1,0:T(8,128)(2,1)} async-done(((bf16[96,2304]{1,0:T(8,128)(2,1)}), bf16[768,2304]{1,0:T(8,128)(2,1)}) %all-gather.10.cloned.1.call-update) | async-done | bytes 3538960 | tf_op jit(solution)/shard_map/all_gather | solution.py:132
  83.3 4.2 fusion.129
  90.0 3.8 all-to-all-start.2
  93.9 32.9 %all_gather.58 = bf16[384,768]{0,1:T(8,128)(2,1)} all-gather(bf16[384,192]{0,1:T(8,128)(2,1)S(1)} %copy-done.26), channel_id=1, replica_groups=mesh['rows'=8,'head'=4] {'head'}, dimensions={1}, use_global_device_ids=true | all-gather | bytes 737280 | tf_op jit(solution)/shard_map/all_gather | solution.py:127
  126.8 5.1 all-gather.3
  131.9 18.8 %all-gather.4 = bf16[8,96,4]{1,2,0:T(4,128)(2,1)S(1)} all-gather(bf16[1,96,4]{1,2,0:T(4,128)(2,1)S(1)} %bitcast.452), channel_id=1, replica_groups=mesh['rows'=8,'head'=4] {'rows'}, dimensions={0}, use_global_device_ids=true | all-gather | bytes 6912 | tf_op jit(solution)/shard_map/all_gather | solution.py:137
  151.4 5.7 fusion.128
  157.1 4.3 copy.135
  161.4 4.5 all-to-all-start
  168.7 23.9 %while.45 = (s32[]{:T(128)}, bf16[4,512,3,64]{1,3,2,0:T(8,128)(2,1)}, f32[4,3,512]{2,1,0:T(4,128)S(1)}, bf16[4,512,3,64]{1,3,2,0:T(8,128)(2,1)S(1)}, s32[4]{0:T(...) while((s32[]{:T(128)}, ...), condition=%wide.region_11.12_spmd, body=%wide.region_8.11_spmd.sunk | while | flops 211385856 | bytes 11335809 | solution.py:190
  194.5 4.4 all-to-all-start.3
  198.9 2.7 slice_bitcast_fusion.3
  202.6 27.6 %while.44 = (s32[]{:T(128)}, bf16[4,512,3,64]{1,3,2,0:T(8,128)(2,1)}, f32[4,3,512]{2,1,0:T(4,128)S(1)}, bf16[4,512,3,64]{1,3,2,0:T(8,128)(2,1)}, s32[4]{0:T(128)...) while((s32[]{:T(128)}, ...), condition=%wide.region_3.4_spmd, body=%wide.region_0.3_spmd.sunk | while | flops 211385856 | bytes 11331713 | solution.py:190
  206.8 2.7 fusion.275
  213.7 2.7 fusion.275
  220.6 2.7 fusion.275
  227.5 2.7 fusion.275
  230.2 4.2 all-to-all-start.1
  234.5 2.7 fusion.199
  237.5 8.6 all-to-all-done.1
  246.1 3.8 fusion.198
  249.9 4.8 fusion.187
  257.4 31.4 %fusion.100 = (bf16[512,3072]{1,0:T(8,128)(2,1)}, bf16[512,3072]{1,0:T(8,128)(2,1)}, f32[512,3072]{1,0:T(8,128)}) fusion(f32[3072]{0:T(1024)S(1)} %add.262, f32[512,3072]{1,0:T(8,128)S(1)} %fusion.187, bf16[768,3072]{1,0:T(8,128)(2,1)S(1)} %copy-done.45, f32[512,768]{1,0:T(8,128)S(1)} %copy-done.20, f32[768]{0:T(1024)S(1)} %get-tuple-element.270, ...), kind=kOutput, calls=%fused_computation.133 | convolution fusion | flops 2625503232 | bytes 25188352 | tf_op jit(solution)/shard_map/dot_general | solution.py:199
  288.9 6.2 fusion.201
  295.5 2.8 fusion.200
  301.0 2.9 fusion.192
  303.9 8.4 fusion.202
  312.3 4.2 multiply_reduce_fusion.3
  316.6 5.0 fusion.203
  321.6 6.3 fusion.197
  333.7 3.0 convolution_convert_fusion.1
  339.0 3.5 all-to-all-start.4
  342.5 2.5 fusion.178
  345.1 3.3 convolution_add_fusion.4
  348.5 5.6 all-to-all-done.4
  354.1 3.5 all-to-all-start.6
  359.3 37.8 %while.46 = (s32[]{:T(128)}, bf16[4,512,3,3,64]{1,4,3,2,0:T(8,128)(2,1)}, bf16[4,512,3,64]{1,3,2,0:T(8,128)(2,1)S(1)}, s32[4]{0:T(128)S(1)}, s32[4]{0:T(128)S(1)...) while((s32[]{:T(128)}, ...), condition=%wide.region_22.23_spmd, body=%wide.region_20.22_spmd.sunk | while | flops 511999488 | bytes 27300500 | solution.py:226
  397.9 3.8 all-to-all-start.5
  403.5 42.0 %while.47 = (s32[]{:T(128)}, bf16[4,512,3,3,64]{1,4,3,2,0:T(8,128)(2,1)}, bf16[4,512,3,64]{1,3,2,0:T(8,128)(2,1)S(1)}, s32[4]{0:T(128)S(1)}, s32[4]{0:T(128)S(1)...) while((s32[]{:T(128)}, ...), condition=%wide.region_29.30_spmd, body=%wide.region_27.29_spmd.sunk | while | flops 511999488 | bytes 30446764 | solution.py:226
  446.9 3.6 all-to-all-start.7
  450.6 6.8 fusion.167
  457.4 21.6 %all-to-all-done.7 = bf16[4,512,1,576]{1,3,2,0:T(8,128)(2,1)S(1)} async-done(((bf16[4,512,1,576]{1,3,2,0:T(8,128)(2,1)}), bf16[4,512,1,576]{1,3,2,0:T(8,128)(2,1)S(1)}, u32[]{:S(2)}, u32[]{:S(2)}) %all-to-all-start.7) | async-done | bytes 2359328 | tf_op jit(solution)/shard_map/all_to_all | solution.py:116
  479.0 8.2 add_bitcast_fusion
  487.2 8.0 copy.160
  495.3 5.2 fusion.181
  500.6 5.6 convolution_add_fusion
  508.9 8.9 fusion.151
  517.9 11.8 convolution_add_fusion.1
  536.8 83.9 %reduce-scatter.31.cloned.1.call-done = f32[96,2304]{1,0:T(8,128)} async-done(((f32[768,2304]{1,0:T(8,128)}), f32[96,2304]{1,0:T(8,128)}) %reduce-scatter.31.cloned.1.call-update) | async-done | bytes 884752
  623.0 162.5 %reduce-scatter.29.cloned.1.call-done = f32[384,768]{1,0:T(8,128)} async-done(((f32[3072,768]{1,0:T(8,128)}), f32[384,768]{1,0:T(8,128)}) %reduce-scatter.29.cloned.1.call-update) | async-done | bytes 1179664 | tf_op jit(solution)/shard_map/reduce_scatter | solution.py:146
  793.9 56.8 %reduce-scatter.39.cloned.1.call-done = f32[96,4]{1,0:T(8,128)} async-done(((f32[768,4]{1,0:T(8,128)}), f32[96,4]{1,0:T(8,128)}) %reduce-scatter.39.cloned.1.call-update) | async-done | bytes 1552
  851.6 163.9 %reduce-scatter.25.cloned.1.call-done = f32[96,3072]{1,0:T(8,128)} async-done(((f32[768,3072]{1,0:T(8,128)}), f32[96,3072]{1,0:T(8,128)}) %reduce-scatter.25.cloned.1.call-update) | async-done | bytes 1179664 | tf_op jit(solution)/shard_map/reduce_scatter | solution.py:145
  1017.7 5.3 add_bitcast_fusion.2
  1027.0 53.0 %reduce-scatter.37.cloned.1.call-done = f32[96,8]{1,0:T(8,128)} async-done(((f32[768,8]{1,0:T(8,128)}), f32[96,8]{1,0:T(8,128)}) %reduce-scatter.37.cloned.1.call-update) | async-done | bytes 3088
  1080.9 5.7 all-reduce.2
  1088.2 13.6 %reduce-scatter.33.cloned.1.call-done = bf16[192,96]{1,0:T(8,128)(2,1)} async-done(((bf16[768,96]{1,0:T(8,128)(2,1)}), bf16[192,96]{1,0:T(8,128)(2,1)}) %reduce-scatter.33.cloned.1.call-update) | async-done | bytes 36880
  1103.4 22.9 %reduce-scatter.21.cloned.1.call-done = bf16[96,576]{0,1:T(8,128)(2,1)} async-done(((bf16[96,2304]{0,1:T(8,128)(2,1)}), bf16[96,576]{0,1:T(8,128)(2,1)}) %reduce-scatter.21.cloned.1.call-update) | async-done | bytes 110608 | tf_op jit(solution)/shard_map/reduce_scatter | solution.py:151
  1128.0 22.8 %reduce-scatter.35.cloned.1.call-done = bf16[192,384]{1,0:T(8,128)(2,1)} async-done(((bf16[768,384]{1,0:T(8,128)(2,1)}), bf16[192,384]{1,0:T(8,128)(2,1)}) %reduce-scatter.35.cloned.1.call-update) | async-done | bytes 147472
  1152.7 22.5 %reduce-scatter.27.cloned.1.call-done = bf16[96,768]{1,0:T(8,128)(2,1)} async-done(((bf16[96,3072]{1,0:T(8,128)(2,1)}), bf16[96,768]{1,0:T(8,128)(2,1)}) %reduce-scatter.27.cloned.1.call-update) | async-done | bytes 147472 | tf_op jit(solution)/shard_map/reduce_scatter | solution.py:157
  (417 shorter events, 188.9 us)
Async XLA Ops:
  7.2 17.8 %copy-start.25 = (bf16[96,768]{1,0:T(8,128)(2,1)S(1)}, bf16[96,768]{1,0:T(8,128)(2,1)}, u32[]{:S(2)}) copy-start(bf16[96,768]{1,0:T(8,128)(2,1)} %param.21) | copy-start | bytes 442372
  7.2 25.9 %copy-start.39 = (bf16[2,96]{1,0:T(2,128)(2,1)S(1)}, bf16[2,96]{1,0:T(2,128)(2,1)}, u32[]{:S(2)}) copy-start(bf16[2,96]{1,0:T(2,128)(2,1)} %param.23) | copy-start | bytes 1156
  7.2 76.1 %all-gather.10.cloned.1.call-start = ((), (), s32[]{:S(2)}) async-start(), calls=%async_computation.18 | async-start | bytes 3981312 | tf_op jit(solution)/shard_map/all_gather | solution.py:132
  17.5 216.9 %all-gather.12.cloned.1.call-start = ((), (), s32[]{:S(2)}) async-start(), calls=%async_computation.19 | async-start | bytes 1327104 | tf_op jit(solution)/shard_map/all_gather | solution.py:133
  24.9 225.0 %all-gather.14.cloned.1.call-start = ((), (), s32[]{:S(2)}) async-start(), calls=%async_computation.20 | async-start | bytes 5308416 | tf_op jit(solution)/shard_map/all_gather | solution.py:134
  90.0 36.8 %copy-start.40 = (bf16[1,96]{1,0:T(2,128)(2,1)S(1)}, bf16[1,96]{1,0:T(2,128)(2,1)}, u32[]{:S(2)}) copy-start(bf16[1,96]{1,0:T(2,128)(2,1)} %param.24) | copy-start | bytes 580
  90.0 61.3 %copy-start.37 = (s32[2,4]{1,0:T(2,128)S(1)}, s32[2,4]{1,0:T(2,128)}, u32[]{:S(2)}) copy-start(s32[2,4]{1,0:T(2,128)} %param.27) | copy-start | bytes 100
  90.0 61.3 %copy-start.38 = (s32[2,4]{1,0:T(2,128)S(1)}, s32[2,4]{1,0:T(2,128)}, u32[]{:S(2)}) copy-start(s32[2,4]{1,0:T(2,128)} %param.26) | copy-start | bytes 100
  90.0 71.3 %all-to-all-start.2 = ((bf16[1,512,4,576]{1,3,0,2:T(8,128)(2,1)}), bf16[1,512,4,576]{1,3,0,2:T(8,128)(2,1)S(1)}, u32[]{:S(2)}, u32[]{:S(2)}) async-start(bf16[1,512,4,576]{1,3,0,2:T(8,128)(2,1)} %bitcast.436), calls=%async_computation.2 | async-start | bytes 4718592 | tf_op jit(solution)/shard_map/all_to_all | solution.py:95
  93.8 195.0 %all-gather.16.cloned.1.call-start = ((), (), s32[]{:S(2)}) async-start(), calls=%async_computation.21 | async-start | bytes 5308416 | tf_op jit(solution)/shard_map/all_gather | solution.py:135
  151.4 144.1 %copy-start.27 = (f32[768]{0:T(1024)}, f32[768]{0:T(1024)S(1)}, u32[]{:S(2)}) copy-start(f32[768]{0:T(1024)S(1)} %get-tuple-element.270) | copy-start | bytes 9220
  161.4 4.6 copy-start.8
  161.4 33.1 %all-to-all-start = ((bf16[1,512,4,576]{1,3,0,2:T(8,128)(2,1)}), bf16[1,512,4,576]{1,3,0,2:T(8,128)(2,1)}, u32[]{:S(2)}, u32[]{:S(2)}) async-start(bf16[1,512,4,576]{1,3,0,2:T(8,128)(2,1)} %bitcast.52), calls=%async_computation | async-start | bytes 4718592 | tf_op jit(solution)/shard_map/all_to_all | solution.py:95
  192.7 6.2 copy-start.16
  192.7 6.2 copy-start.24
  192.7 6.2 copy-start.41
  192.7 6.2 copy-start.43
  192.7 9.0 copy-start.1
  192.7 9.0 copy-start.3
  194.5 35.7 %all-to-all-start.3 = ((bf16[4,512,1,192]{1,3,2,0:T(8,128)(2,1)}), bf16[4,512,1,192]{1,3,2,0:T(8,128)(2,1)}, u32[]{:S(2)}, u32[]{:S(2)}) async-start(bf16[4,512,1,192]{1,3,2,0:T(8,128)(2,1)} %bitcast.85), calls=%async_computation.3 | async-start | bytes 1572864 | tf_op jit(solution)/shard_map/all_to_all | solution.py:101
  230.2 4.2 copy-start.23
  230.2 15.9 %all-to-all-start.1 = ((bf16[4,512,1,192]{1,3,2,0:T(8,128)(2,1)}), bf16[4,512,1,192]{1,3,2,0:T(8,128)(2,1)}, u32[]{:S(2)}, u32[]{:S(2)}) async-start(bf16[4,512,1,192]{1,3,2,0:T(8,128)(2,1)} %bitcast.63), calls=%async_computation.1 | async-start | bytes 1572864 | tf_op jit(solution)/shard_map/all_to_all | solution.py:101
  237.2 90.8 %copy-start.5 = (f32[512,768]{1,0:T(8,128)}, f32[512,768]{1,0:T(8,128)S(1)}, u32[]{:S(2)}) copy-start(f32[512,768]{1,0:T(8,128)S(1)} %get-tuple-element.390) | copy-start | bytes 4718596
  249.9 4.9 copy-start.20
  249.9 7.5 copy-start.45
  257.4 31.5 %copy-start.36 = (f32[768]{0:T(1024)S(1)}, f32[768]{0:T(1024)}, u32[]{:S(2)}) copy-start(f32[768]{0:T(1024)} %get-tuple-element.264) | copy-start | bytes 9220
  288.9 6.6 copy-start.17
  288.9 6.6 copy-start.21
  288.9 6.6 copy-start.46
  300.9 11.4 slice-start
  300.9 15.6 %slice-start.2 = ((s8[6291456]{0:T(1024)(128)(4,1)}), s8[4194304]{0:T(1024)(128)(4,1)S(1)}, s32[]{:S(2)}) async-start(s8[6291456]{0:T(1024)(128)(4,1)} %bitcast.457), calls=%async_computation.34 | async-start | bytes 8388608
  303.9 8.5 copy-start.12
  303.9 17.7 %copy-start.10 = (f32[512,768]{1,0:T(8,128)}, f32[512,768]{1,0:T(8,128)S(1)}, u32[]{:S(2)}) copy-start(f32[512,768]{1,0:T(8,128)S(1)} %get-tuple-element.343) | copy-start | bytes 4718596
  303.9 8.5 slice-start.1
  303.9 12.7 %slice-start.3 = ((s8[6291456]{0:T(1024)(128)(4,1)}), s8[2097152]{0:T(1024)(128)(4,1)S(1)}, s32[]{:S(2)}) async-start(s8[6291456]{0:T(1024)(128)(4,1)} %bitcast.457), calls=%async_computation.35 | async-start | bytes 4194304
  321.6 6.4 copy-start.18
  328.5 5.2 copy-start.22
  339.0 15.1 %all-to-all-start.4 = ((bf16[1,512,4,192]{1,3,0,2:T(8,128)(2,1)}), bf16[1,512,4,192]{1,3,0,2:T(8,128)(2,1)S(1)}, u32[]{:S(2)}, u32[]{:S(2)}) async-start(bf16[1,512,4,192]{1,3,0,2:T(8,128)(2,1)} %bitcast.92), calls=%async_computation.4 | async-start | bytes 1572864 | tf_op jit(solution)/shard_map/all_to_all | solution.py:110
  342.5 192.4 %reduce-scatter.23.cloned.1.call-start = ((), (), s32[]{:S(2)}) async-start(), calls=%async_computation.23 | async-start | bytes 2654208 | tf_op jit(solution)/shard_map/reduce_scatter | solution.py:144
  354.1 43.0 %all-to-all-start.6 = ((bf16[1,512,4,192]{1,3,0,2:T(8,128)(2,1)}), bf16[1,512,4,192]{1,3,0,2:T(8,128)(2,1)S(1)}, u32[]{:S(2)}, u32[]{:S(2)}) async-start(bf16[1,512,4,192]{1,3,0,2:T(8,128)(2,1)} %bitcast.437), calls=%async_computation.6 | async-start | bytes 1572864 | tf_op jit(solution)/shard_map/all_to_all | solution.py:110
  397.0 6.5 copy-start.2
  397.0 6.5 copy-start.42
  397.0 6.5 copy-start.44
  397.9 47.6 %all-to-all-start.5 = ((bf16[4,512,1,576]{1,3,2,0:T(8,128)(2,1)}), bf16[4,512,1,576]{1,3,2,0:T(8,128)(2,1)S(1)}, u32[]{:S(2)}, u32[]{:S(2)}) async-start(bf16[4,512,1,576]{1,3,2,0:T(8,128)(2,1)} %bitcast.97), calls=%async_computation.5 | async-start | bytes 4718592 | tf_op jit(solution)/shard_map/all_to_all | solution.py:116
  403.5 5.1 copy-start.4
  414.0 5.1 copy-start.4
  424.4 5.1 copy-start.4
  435.0 5.1 copy-start.4
  446.9 32.1 %all-to-all-start.7 = ((bf16[4,512,1,576]{1,3,2,0:T(8,128)(2,1)}), bf16[4,512,1,576]{1,3,2,0:T(8,128)(2,1)S(1)}, u32[]{:S(2)}, u32[]{:S(2)}) async-start(bf16[4,512,1,576]{1,3,2,0:T(8,128)(2,1)} %bitcast.109), calls=%async_computation.7 | async-start | bytes 4718592 | tf_op jit(solution)/shard_map/all_to_all | solution.py:116
  450.6 170.1 %reduce-scatter.31.cloned.1.call-start = ((), (), s32[]{:S(2)}) async-start(), calls=%async_computation.27 | async-start | bytes 7962624
  495.2 290.3 %reduce-scatter.29.cloned.1.call-start = ((), (), s32[]{:S(2)}) async-start(), calls=%async_computation.26 | async-start | bytes 10616832 | tf_op jit(solution)/shard_map/reduce_scatter | solution.py:146
  495.3 5.3 copy-start.9
  495.3 5.3 copy-start.11
  506.2 344.5 %reduce-scatter.39.cloned.1.call-start = ((), (), s32[]{:S(2)}) async-start(), calls=%async_computation.31 | async-start | bytes 442368
  517.9 497.6 %reduce-scatter.25.cloned.1.call-start = ((), (), s32[]{:S(2)}) async-start(), calls=%async_computation.24 | async-start | bytes 10616832 | tf_op jit(solution)/shard_map/reduce_scatter | solution.py:145
  529.7 550.3 %reduce-scatter.37.cloned.1.call-start = ((), (), s32[]{:S(2)}) async-start(), calls=%async_computation.30 | async-start | bytes 442368
  534.8 567.1 %reduce-scatter.33.cloned.1.call-start = ((), (), s32[]{:S(2)}) async-start(), calls=%async_computation.28 | async-start | bytes 245760
  535.9 254.3 %copy-start.49 = (u32[32]{0:T(128)S(1)}, u32[32]{0:T(128)}, u32[]{:S(2)}) copy-start(u32[32]{0:T(128)} %constant.177) | copy-start | bytes 388
  535.9 255.6 %copy-start.19 = (bf16[1,1,512,768]{3,2,1,0:T(8,128)(2,1)S(1)}, bf16[1,1,512,768]{3,2,1,0:T(8,128)(2,1)}, u32[]{:S(2)}) copy-start(bf16[1,1,512,768]{3,2,1,0:T(8,128)(2,1)} %get-tuple-element.373) | copy-start | bytes 2359300
  536.7 589.6 %reduce-scatter.21.cloned.1.call-start = ((), (), s32[]{:S(2)}) async-start(), calls=%async_computation.22 | async-start | bytes 737280 | tf_op jit(solution)/shard_map/reduce_scatter | solution.py:151
  623.0 527.9 %reduce-scatter.35.cloned.1.call-start = ((), (), s32[]{:S(2)}) async-start(), calls=%async_computation.29 | async-start | bytes 737280
  789.9 385.4 %reduce-scatter.27.cloned.1.call-start = ((), (), s32[]{:S(2)}) async-start(), calls=%async_computation.25 | async-start | bytes 737280 | tf_op jit(solution)/shard_map/reduce_scatter | solution.py:157
  1017.7 5.4 copy-start.15
  1017.7 5.4 copy-start.47
  (17 other events, 35.8 us)
Sparse Core Ops, SparseCore 0:
  17.6 65.6 all-gather.9
  86.1 39.7 all-gather.11
  128.1 78.0 all-gather.13
  208.1 78.9 all-gather.15
  348.6 67.5 reduce-scatter.22
  495.3 125.2 reduce-scatter.30
  624.3 161.2 reduce-scatter.28
  789.4 61.2 reduce-scatter.38
  854.3 161.1 reduce-scatter.24
  1018.6 61.3 reduce-scatter.36
  1083.0 18.7 reduce-scatter.32
  1104.2 22.0 reduce-scatter.20
  1128.8 22.0 reduce-scatter.34
  1153.2 22.0 reduce-scatter.26
where the time goes:
time: 1190 us; the launch traced here: 1180 us
  waiting for transfers between devices  657 us (55%)
  matrix products  213 us (18%)
  blocking collectives  117 us (10%)
  local copies, waits for them, and re-layouts  79.6 us (7%)
  other arithmetic  68.8 us (6%)
  starting transfers between devices  32.3 us (3%)
  between operations  16 us (1%)
    unnamed x19, waiting for transfers between devices  230 us
    reduce_scatter x1, waiting for transfers between devices, reduce_grads(): lax.psum_scatter(running[2], 'rows', scatter_dimension=0, tiled=True)  164 us
    reduce_scatter x1, waiting for transfers between devices, reduce_grads(): lax.psum_scatter(running[3], 'rows', scatter_dimension=0, tiled=True)  163 us
    dot_general x8, matrix products, contract_rows(): lax.dot_general(left, right, (((0,), (0,)), ((), ())), preferred_element_...  52.4 us
    dot_general x2, matrix products, layer_step(): jnp.dot(hidden_low, up_full, preferred_element_type=jnp.float32)  36.3 us
    dot_general x8, matrix products, contract_cols(): lax.dot_general(left, right, (((1,), (1,)), ((), ())), preferred_element_...  36.1 us
    all_gather x1, blocking collectives, gather_weights(): lax.all_gather(down_weight, 'head', axis=1, tiled=True)  32.9 us
    unnamed x126, local copies, waits for them, and re-layouts  30.5 us
  transfers between devices with their start and end apart: 22, of which 14 were waited for; matrix products, arithmetic and copies ran while one was open for 26% of the time, Pallas kernels for 0%

commit v1 on v0

v1 whole, which is shorter than its diff:
```python
import jax
import jax.numpy as jnp
from jax import lax
from jax.sharding import PartitionSpec as P

HD = 64
EPSILON = 1e-06
ROOT_HALF = 0.7071067811865476
INVERSE_ROOT_TWO_PI = 0.3989422804014327
AXES = ("rows", "head")


def contract_rows(left, right):
    return lax.dot_general(
        left, right, (((0,), (0,)), ((), ())), preferred_element_type=jnp.float32
    )


def contract_cols(left, right):
    return lax.dot_general(
        left, right, (((1,), (1,)), ((), ())), preferred_element_type=jnp.float32
    )


def norm_forward(values_in, gain_row, shift_row):
    average = jnp.mean(values_in, axis=-1, keepdims=True)
    centered = values_in - average
    variance = jnp.mean(centered * centered, axis=-1, keepdims=True)
    inverse_scale = lax.rsqrt(variance + EPSILON)
    normed = centered * inverse_scale
    return (normed * gain_row + shift_row, normed, inverse_scale)


def norm_backward(grad_out, normed, inverse_scale, gain_row):
    grad_normed = grad_out * gain_row
    first_mean = jnp.mean(grad_normed, axis=-1, keepdims=True)
    second_mean = jnp.mean(grad_normed * normed, axis=-1, keepdims=True)
    grad_in = inverse_scale * (grad_normed - first_mean - normed * second_mean)
    return (grad_in, jnp.sum(grad_out * normed, axis=0), jnp.sum(grad_out, axis=0))


def masked_scores(queries, keys_in, bound, length):
    seq = queries.shape[0]
    positions = lax.broadcasted_iota(jnp.int32, (seq,), 0)
    segment = positions >= bound
    allowed = (segment[:, None] == segment[None, :]) & (positions[None, :] < length)
    scores = jnp.einsum(
        "qhe,khe->hqk", queries, keys_in, preferred_element_type=jnp.float32
    ) * HD ** (-0.5)
    return jnp.where(allowed[None], scores, -1e30)


def attend_forward(queries, keys_in, values_in, bound, length):
    scores = masked_scores(queries, keys_in, bound, length)
    highest = jnp.max(scores, axis=-1, keepdims=True)
    raised = jnp.exp(scores - highest)
    totals = jnp.sum(raised, axis=-1, keepdims=True)
    weights_low = (raised / totals).astype(jnp.bfloat16)
    context = jnp.einsum("hqk,khe->qhe", weights_low, values_in, preferred_element_type=jnp.float32)
    log_total = (highest + jnp.log(totals))[..., 0]
    return (context.astype(jnp.bfloat16), log_total)


def attend_backward(queries, keys_in, values_in, bound, length, log_total, grad_context):
    scores = masked_scores(queries, keys_in, bound, length)
    weights_full = jnp.exp(scores - log_total[..., None])
    weights_low = weights_full.astype(jnp.bfloat16)
    grad_values = jnp.einsum(
        "hqk,qhe->khe", weights_low, grad_context, preferred_element_type=jnp.float32
    )
    grad_weights = jnp.einsum(
        "qhe,khe->hqk", grad_context, values_in, preferred_element_type=jnp.float32
    )
    inner_sum = jnp.sum(weights_full * grad_weights, axis=-1, keepdims=True)
    grad_scores = (weights_full * (grad_weights - inner_sum)).astype(jnp.bfloat16)
    grad_queries = jnp.einsum(
        "hqk,khe->qhe", grad_scores, keys_in, preferred_element_type=jnp.float32
    ) * HD ** (-0.5)
    grad_keys = jnp.einsum(
        "hqk,qhe->khe", grad_scores, queries, preferred_element_type=jnp.float32
    ) * HD ** (-0.5)
    return jnp.stack([grad_queries, grad_keys, grad_values], axis=2).astype(jnp.bfloat16)


def gather(shard, row_axis):
    rows, head = lax.axis_size("rows"), lax.axis_size("head")
    a, b = shard.shape
    every = lax.all_gather(shard, AXES, axis=0, tiled=False).reshape(rows, head, a, b)
    if row_axis == 0:
        return every.transpose(0, 2, 1, 3).reshape(rows * a, head * b)
    return every.transpose(1, 2, 0, 3).reshape(head * a, rows * b)


def scatter(grad, row_axis):
    rows, head = lax.axis_size("rows"), lax.axis_size("head")
    a, b = grad.shape
    if row_axis == 0:
        parts = grad.reshape(rows, a // rows, head, b // head).transpose(0, 2, 1, 3)
    else:
        parts = grad.reshape(head, a // head, rows, b // rows).transpose(2, 0, 1, 3)
    parts = parts.reshape((rows * head,) + parts.shape[2:]).astype(jnp.bfloat16)
    return lax.psum_scatter(parts, AXES, scatter_dimension=0, tiled=False).astype(jnp.float32)


def shards(
    inputs,
    qkv_weight,
    out_weight,
    up_weight,
    down_weight,
    biases,
    norm_params,
    cotangent,
    boundaries,
    lengths,
):
    micro, seq_per, seq, width = inputs.shape
    count = micro * seq_per
    heads = width // HD
    qkv_full, out_full, up_full, down_full = (
        gather(w, 0) for w in (qkv_weight, out_weight, up_weight, down_weight)
    )
    bias_float = gather(biases, 1).astype(jnp.float32)
    norm_float = gather(norm_params, 1).astype(jnp.float32)
    first_seq = lax.axis_index("head") * seq_per
    bounds = lax.dynamic_slice_in_dim(boundaries, first_seq, seq_per, 1).reshape(count)
    lens = lax.dynamic_slice_in_dim(lengths, first_seq, seq_per, 1).reshape(count)

    tokens = inputs.reshape(count * seq, width)
    zero_part = jnp.zeros((heads, HD), jnp.float32)
    head_bias = jnp.stack(
        [bias_float[0].reshape(heads, HD), zero_part, bias_float[1].reshape(heads, HD)], axis=1
    ).reshape(3 * width)
    project = (jnp.dot(tokens, qkv_full, preferred_element_type=jnp.float32) + head_bias).astype(
        jnp.bfloat16
    )
    items = project.reshape(count, seq, heads, 3, HD)
    q, k, v = items[:, :, :, 0], items[:, :, :, 1], items[:, :, :, 2]
    context, log_total = jax.vmap(attend_forward)(q, k, v, bounds, lens)
    context = context.reshape(count * seq, width)
    attended = jnp.dot(context, out_full, preferred_element_type=jnp.float32) + bias_float[2]
    hidden, normed_one, scale_one = norm_forward(
        tokens.astype(jnp.float32) + attended, norm_float[0], norm_float[1]
    )
    hidden_low = hidden.astype(jnp.bfloat16)
    inner_pre = jnp.dot(hidden_low, up_full, preferred_element_type=jnp.float32) + bias_float[
        4:8
    ].reshape(-1)
    cdf = 0.5 * (1.0 + lax.erf(inner_pre * ROOT_HALF))
    active_low = (inner_pre * cdf).astype(jnp.bfloat16)
    slope = cdf + inner_pre * jnp.exp(-0.5 * inner_pre * inner_pre) * INVERSE_ROOT_TWO_PI
    outer_out = jnp.dot(active_low, down_full, preferred_element_type=jnp.float32) + bias_float[3]
    output_float, normed_two, scale_two = norm_forward(
        hidden + outer_out, norm_float[2], norm_float[3]
    )
    grad_out = cotangent.reshape(count * seq, width).astype(jnp.float32)
    grad_two, gain_two, shift_two = norm_backward(grad_out, normed_two, scale_two, norm_float[2])
    grad_two_low = grad_two.astype(jnp.bfloat16)
    down_grad = scatter(contract_rows(active_low, grad_two_low), 0)
    grad_inner = contract_cols(grad_two_low, down_full) * slope
    grad_inner_low = grad_inner.astype(jnp.bfloat16)
    up_grad = scatter(contract_rows(hidden_low, grad_inner_low), 0)
    grad_hidden = contract_cols(grad_inner_low, up_full) + grad_two
    grad_one, gain_one, shift_one = norm_backward(grad_hidden, normed_one, scale_one, norm_float[0])
    grad_one_low = grad_one.astype(jnp.bfloat16)
    out_grad = scatter(contract_rows(context, grad_one_low), 0)
    grad_context = contract_cols(grad_one_low, out_full).astype(jnp.bfloat16)
    grad_items = grad_context.reshape(count, seq, heads, HD)
    grad_project = jax.vmap(attend_backward)(q, k, v, bounds, lens, log_total, grad_items)
    grad_project = grad_project.reshape(count * seq, 3 * width)
    qkv_grad = scatter(contract_rows(tokens, grad_project), 0)
    grad_input = contract_cols(grad_project, qkv_full) + grad_one
    project_sums = jnp.sum(grad_project, axis=0, dtype=jnp.float32).reshape(heads, 3, HD)
    bias_grad = jnp.concatenate(
        [
            project_sums[:, 0].reshape(1, width),
            project_sums[:, 2].reshape(1, width),
            jnp.sum(grad_one, axis=0).reshape(1, width),
            jnp.sum(grad_two, axis=0).reshape(1, width),
            jnp.sum(grad_inner, axis=0).reshape(4, width),
        ],
        axis=0,
    )
    norm_grad = jnp.stack([gain_one, shift_one, gain_two, shift_two])
    return (
        output_float.astype(jnp.bfloat16).reshape(inputs.shape),
        grad_input.reshape(inputs.shape),
        qkv_grad,
        out_grad,
        up_grad,
        down_grad,
        scatter(bias_grad, 1),
        scatter(norm_grad, 1),
    )


def solution(mesh):
    tokens = P(None, ("rows", "head"), None, None)
    weight = P("rows", "head")
    small = P("head", "rows")
    per_row = P(None, "rows")
    return jax.shard_map(
        shards,
        mesh=mesh,
        in_specs=(tokens, weight, weight, weight, weight, small, small, tokens, per_row, per_row),
        out_specs=(tokens, tokens, weight, weight, weight, weight, small, small),
        check_vma=False,
    )
```

time: 1190 us -> 821 us (0.69)
  waiting for transfers between devices: 657 us -> 309 us
  local copies, waits for them, and re-layouts: 79.6 us -> 142 us
  matrix products: 213 us -> 170 us
  starting transfers between devices: 32.3 us -> 0.31 us
  other arithmetic: 68.8 us -> 54.7 us
    unnamed x19 -> x8, waiting for transfers between devices: 230 us -> 2.65 us
    reduce_scatter x5 -> x4, waiting for transfers between devices: 372 us -> 244 us  [scatter(): lax.psum_scatter(parts, AXES, scatter_dimension=0, tiled=False)]
    reshape x8 -> x12, local copies, waits for them, and re-layouts: 0.21 us -> 47.2 us  [the longest x5 25.2 us: gather(): lax.all_gather(shard, AXES, axis=0, tiled=False).reshape(rows, head, a, b)]
    all_gather x4, waiting for transfers between devices: 16.8 us -> 62.1 us  [gather(): lax.all_gather(shard, AXES, axis=0, tiled=False).reshape(rows, head, a, b)]
    convert_element_type x7 -> x16, local copies, waits for them, and re-layouts: 11.5 us -> 50.8 us  [the longest x11 39.9 us: scatter(): parts = parts.reshape((rows * head,) + parts.shape[2:]).astype(jnp.bfloat16)]
    all_to_all x8 -> x0, waiting for transfers between devices: 37.7 us -> none  [the longest x2 21.6 us: grad_to_tokens(): lax.all_to_all(grad_items.reshape(-1, SEQ, 1, width), 'head', split_axis=...]
    dot_general x8 -> x4, matrix products: 61.7 us -> 24.3 us  [the longest x1 9.75 us: shards(): jnp.dot(hidden_low, up_full, preferred_element_type=jnp.float32)]
    unnamed x1, blocking collectives: 5.65 us -> 38.8 us
  transfers between devices with their start and end apart: 22 -> 8, of which waited for: 14 -> 5; matrix products, arithmetic and copies ran while one was open for 26% -> 30% of each run, Pallas kernels for 0% -> 0%
where the time goes in v1:
time: 821 us; the launch traced here: 809 us
  waiting for transfers between devices  309 us (38%)
  matrix products  170 us (21%)
  local copies, waits for them, and re-layouts  142 us (17%)
  blocking collectives  119 us (14%)
  other arithmetic  54.7 us (7%)
  between operations  14.8 us (2%)
    reduce_scatter x4, waiting for transfers between devices, scatter(): lax.psum_scatter(parts, AXES, scatter_dimension=0, tiled=False)  244 us
    all_gather x2, blocking collectives, gather(): lax.all_gather(shard, AXES, axis=0, tiled=False).reshape(rows, head, a, b)  80.3 us
    all_gather x4, waiting for transfers between devices, gather(): lax.all_gather(shard, AXES, axis=0, tiled=False).reshape(rows, head, a, b)  62.1 us
    convert_element_type x11, local copies, waits for them, and re-layouts, scatter(): parts = parts.reshape((rows * head,) + parts.shape[2:]).astype(jnp.bfloat16)  39.9 us
    unnamed x1, blocking collectives  38.8 us
    dot_general x4, matrix products, contract_cols(): lax.dot_general(left, right, (((1,), (1,)), ((), ())), preferred_element_...  36.4 us
    dot_general x4, matrix products, contract_rows(): lax.dot_general(left, right, (((0,), (0,)), ((), ())), preferred_element_...  30 us
    reshape x5, local copies, waits for them, and re-layouts, gather(): lax.all_gather(shard, AXES, axis=0, tiled=False).reshape(rows, head, a, b)  25.2 us
  transfers between devices with their start and end apart: 8, of which 5 were waited for; matrix products, arithmetic and copies ran while one was open for 30% of the time, Pallas kernels for 0%

profile of v1, /device:TPU:0, one launch (start us, length us, event | category | flops | bytes accessed | tf_op | source)
XLA Modules:
  0.0 809.3 jit_solution(16634827695324062323)
XLA Ops:
  10.0 43.5 %all-gather.6 = bf16[32,2,96]{2,1,0:T(2,128)(2,1)S(1)} all-gather(bf16[1,2,96]{2,1,0:T(2,128)(2,1)} %bitcast.227), channel_id=3, replica_groups=mesh['rows'=8,'head'=4] {'rows','head'}, dimensions={0}, use_global_device_ids=true | all-gather | bytes 12672 | tf_op jit(solution)/shard_map/all_gather | solution.py:88
  55.2 36.8 %all-gather.7 = bf16[32,1,96]{2,1,0:T(2,128)(2,1)S(1)} all-gather(bf16[1,1,96]{2,1,0:T(2,128)(2,1)} %bitcast.228), channel_id=5, replica_groups=mesh['rows'=8,'head'=4] {'rows','head'}, dimensions={0}, use_global_device_ids=true | all-gather | bytes 6336 | tf_op jit(solution)/shard_map/all_gather | solution.py:88
  92.3 1.8 fusion.18
  94.7 2.1 copy.97
  98.1 33.3 %all-gather.13.cloned.1.call-done = bf16[3072,576]{1,0:T(8,128)(2,1)} async-done(((bf16[96,576]{1,0:T(8,128)(2,1)}), bf16[3072,576]{1,0:T(8,128)(2,1)}) %all-gather.13.cloned.1.call-update) | async-done | bytes 3538960 | tf_op jit(solution)/shard_map/all_gather | solution.py:88
  131.5 6.0 copy.157
  137.5 8.0 reshape.314
  145.5 7.5 add_convert_fusion
  152.9 6.6 copy.91
  159.6 8.9 %reshape.315 = bf16[2,512,12,3,64]{1,0,4,3,2:T(2,128)(2,1)} reshape(bf16[1024,2304]{0,1:T(8,128)(2,1)} %copy.91) | data formatting | bytes 9437184 | tf_op jit(solution)/shard_map/reshape | solution.py:137
  168.5 4.9 fusion.59
  173.4 10.9 %fusion.11 = (f32[2,12,512]{2,1,0:T(8,128)S(1)}, f32[2,12,512,512]{2,3,1,0:T(8,128)}) fusion(pred[2,512,512]{1,2,0:T(8,128)(4,1)S(1)} %compare_and_fusion, bf16[2,512,12,1,64]{1,0,4,3,2:T(2,128)(2,1)S(1)} %get-tuple-element.64, bf16[2,512,12,1,64]{1,0,4,3,2:T(2,128)(2,1)S(1)} %get-tuple-element.63), kind=kOutput, calls=%fused_computation.20 | convolution fusion | flops 824168448 | bytes 28884992 | tf_op jit(solution)/shard_map/vmap(qhe,khe->hqk)/dot_general | solution.py:47
  184.3 11.1 %fusion = f32[2,12,512]{2,1,0:T(8,128)S(1)} fusion(f32[2,12,512]{2,1,0:T(8,128)S(1)} %get-tuple-element.68, f32[2,12,512,512]{2,3,1,0:T(8,128)} %get-tuple-element.69, pred[2,512,512]{1,2,0:T(8,128)(4,1)S(1)} %compare_and_fusion), kind=kLoop, calls=%fused_computation.6 | loop fusion | flops 25153536 | bytes 25788416 | tf_op jit(solution)/shard_map/vmap()/reduce_sum | solution.py:57
  195.4 22.2 %fusion.36 = bf16[2,512,12,64]{1,3,2,0:T(8,128)(2,1)S(1)} fusion(f32[2,12,512]{2,1,0:T(8,128)S(1)} %fusion, f32[2,12,512]{2,1,0:T(8,128)S(1)} %get-tuple-element.68, f32[2,12,512,512]{2,3,1,0:T(8,128)} %get-tuple-element.69, pred[2,512,512]{1,2,0:T(8,128)(4,1)S(1)} %compare_and_fusion, bf16[2,512,12,1,64]{1,0,4,3,2:T(2,128)(2,1)S(1)} %get-tuple-element.62), kind=kOutput, calls=%fused_computation.68 | convolution fusion | flops 837550080 | bytes 28934144 | tf_op jit(solution)/shard_map/vmap(hqk,khe->qhe)/dot_general | solution.py:59
  217.7 1.6 copy.96
  219.7 1.6 fusion.61
  221.4 1.6 copy-done.7
  223.6 6.0 copy.98
  229.6 3.2 copy.129
  232.8 28.7 %all-gather.19.cloned.1.call-done = bf16[12288,192]{0,1:T(8,128)(2,1)} async-done(((bf16[384,192]{0,1:T(8,128)(2,1)}), bf16[12288,192]{0,1:T(8,128)(2,1)}) %all-gather.19.cloned.1.call-update) | async-done | bytes 4718608 | tf_op jit(solution)/shard_map/all_gather | solution.py:88
  261.5 8.2 %reshape.321 = bf16[8,4,384,192]{2,1,0,3:T(4,128)(2,1)} reshape(bf16[12288,192]{0,1:T(8,128)(2,1)} %all-gather.19.cloned.1.call-done) | data formatting | bytes 9437184 | tf_op jit(solution)/shard_map/reshape | solution.py:88
  269.6 2.9 copy.99
  275.9 9.8 %multiply_convert_fusion.1 = (bf16[1024,3072]{1,0:T(8,128)(2,1)S(1)}, f32[1024,3072]{1,0:T(8,128)}) fusion(f32[3072]{0:T(1024)S(1)} %add.133, bf16[768,3072]{1,0:T(8,128)(2,1)S(1)} %bitcast.208, f32[1024,768]{1,0:T(8,128)S(1)} %copy-done.8, f32[768]{0:T(1024)S(1)} %add.130, f32[768]{0:T(1024)S(1)} %mul.161, f32[1024]{0:T(1024)S(1)} %add_rsqrt_fusion.1, ...), kind=kOutput, calls=%fused_computation.16 | convolution fusion | flops 4854644736 | bytes 26765312 | tf_op jit(solution)/shard_map/dot_general | solution.py:146
  285.6 5.5 fusion.62
  292.6 1.8 fusion.19
  294.3 2.8 fusion.55
  297.2 14.9 %fusion.63 = (bf16[3072]{0:T(1024)(128)(2,1)}, bf16[1024,3072]{1,0:T(8,128)(2,1)}) fusion(f32[1024,3072]{1,0:T(8,128)} %get-tuple-element.73, f32[3072]{0:T(1024)S(1)} %add.133, bf16[3072,768]{0,1:T(8,128)(2,1)S(1)} %bitcast.211, f32[1024,768]{1,0:T(8,128)S(1)} %get-tuple-element.57), kind=kOutput, calls=%fused_computation.123 | convolution fusion | flops 4870370304 | bytes 26757120 | tf_op jit(solution)/shard_map/dot_general | solution.py:20
  312.0 8.9 %multiply_reduce_fusion.1 = (bf16[768]{0:T(1024)(128)(2,1)}, f32[1024]{0:T(1024)S(1)}, f32[1024]{0:T(1024)S(1)}, bf16[768]{0:T(1024)(128)(2,1)}, f32[1024,768]{1,0:T(8,128)S(1)}) fusion(f32[1024,768]{1,0:T(8,128)S(1)} %copy-done.8, f32[1024]{0:T(1024)S(1)} %add_rsqrt_fusion.1, f32[1024]{0:T(1024)S(1)} %broadcast_multiply_fusion.4, f32[768]{0:T(1024)S(1)} %mul.161, ...), kind=kOutput, calls=%fused_computation.37 | convolution fusion | flops 4839698432 | bytes 20469760 | tf_op jit(solution)/shard_map/dot_general | solution.py:20
  320.9 1.9 fusion.57
  322.8 2.5 convolution_convert_fusion.4
  326.7 2.6 copy.100
  329.3 3.9 reshape.324
  333.1 12.6 %fusion.31 = bf16[2,512,12,1,64]{1,4,2,0,3:T(8,128)(2,1)} fusion(f32[2,12,512]{2,1,0:T(8,128)S(1)} %log_add_fusion, f32[2,12,512,512]{2,3,1,0:T(8,128)} %get-tuple-element.69, pred[2,512,512]{1,2,0:T(8,128)(4,1)S(1)} %compare_and_fusion, bf16[2,512,12,64]{1,0,3,2:T(2,128)(2,1)} %reshape.324), kind=kOutput, calls=%fused_computation.65 | convolution fusion | flops 831258624 | bytes 28884992 | tf_op jit(solution)/shard_map/vmap(hqk,qhe->khe)/dot_general | solution.py:68
  345.7 18.0 %multiply_reduce_fusion = (f32[2,12,512]{2,1,0:T(8,128)S(1)}, f32[2,12,512,512]{2,3,1,0:T(8,128)}) fusion(f32[2,12,512]{2,1,0:T(8,128)S(1)} %log_add_fusion, f32[2,12,512,512]{2,3,1,0:T(8,128)} %get-tuple-element.69, pred[2,512,512]{1,2,0:T(8,128)(4,1)S(1)} %compare_and_fusion, bf16[2,512,12,1,64]{1,0,4,3,2:T(2,128)(2,1)S(1)} %get-tuple-element.62, ...), kind=kOutput, calls=%fused_computation.1 | convolution fusion | flops 836751360 | bytes 54099968 | tf_op jit(solution)/shard_map/vmap(qhe,khe->hqk)/dot_general | solution.py:71
  363.7 2.7 copy.109
  366.4 4.4 convolution_convert_fusion.3
  370.8 21.9 %multiply_convert_fusion = bf16[2,12,512,512]{2,3,1,0:T(8,128)(2,1)} fusion(f32[2,12,512,512]{2,3,1,0:T(8,128)} %get-tuple-element.78, f32[2,12,512]{2,1,0:T(8,128)S(1)} %get-tuple-element.77, f32[2,12,512]{2,1,0:T(8,128)S(1)} %log_add_fusion, f32[2,12,512,512]{2,3,1,0:T(8,128)} %get-tuple-element.69, pred[2,512,512]{1,2,0:T(8,128)(4,1)S(1)} %compare_and_fusion), kind=kLoop, calls=%fused_computation | loop fusion | flops 37748736 | bytes 63537152 | tf_op jit(solution)/shard_map/vmap()/convert_element_type | solution.py:75
  392.8 8.7 %fusion.35 = bf16[2,512,12,1,64]{1,4,2,0,3:T(8,128)(2,1)S(1)} fusion(bf16[2,12,512,512]{2,3,1,0:T(8,128)(2,1)} %multiply_convert_fusion, bf16[2,512,12,1,64]{1,0,4,3,2:T(2,128)(2,1)S(1)} %copy-done.5), kind=kOutput, calls=%fused_computation.67 | convolution fusion | flops 806879232 | bytes 15728640 | tf_op jit(solution)/shard_map/vmap(hqk,qhe->khe)/dot_general | solution.py:79
  401.5 6.9 fusion.34
  408.5 2.6 fusion.58
  411.0 9.4 %copy.106 = bf16[2,512,12,3,64]{1,0,4,3,2:T(2,128)(2,1)} copy(bf16[2,512,12,3,64]{1,4,2,0,3:T(8,128)(2,1)} %get-tuple-element.61) | data formatting | bytes 9437184 | tf_op jit(solution)/shard_map/vmap()/stack | solution.py:82
  420.5 4.0 copy.132
  424.4 2.1 copy-done.10
  426.6 5.7 fusion.12
  432.2 4.3 copy.107
  436.6 5.7 convert_element_type.238
  442.3 4.7 copy.108
  447.1 1.8 copy-done.9
  448.9 9.9 %convolution_convert_fusion.1 = bf16[768,3072]{1,0:T(8,128)(2,1)} fusion(bf16[1024,3072]{1,0:T(8,128)(2,1)} %get-tuple-element.80, f32[1024,768]{1,0:T(8,128)S(1)} %copy-done.9, f32[768]{0:T(1024)S(1)} %copy-done.26, f32[768]{0:T(1024)S(1)} %copy-done.18, f32[1024]{0:T(1024)S(1)} %copy-done.20, f32[1024]{0:T(1024)S(1)} %broadcast_multiply_fusion.4), kind=kOutput, calls=%fused_computation.22 | convolution fusion | flops 4838129664 | bytes 14170112 | tf_op jit(solution)/shard_map/dot_general | solution.py:14
  458.8 9.7 %convert_element_type.249 = bf16[8,96,4,768]{3,2,1,0:T(4,128)(2,1)} reshape(bf16[768,3072]{1,0:T(8,128)(2,1)} %convolution_convert_fusion.1) | data formatting | bytes 9437184 | tf_op jit(solution)/shard_map/convert_element_type | solution.py:101
  468.6 5.4 copy.110
  474.0 1.8 copy-done.13
  475.8 10.0 %convolution_convert_fusion = bf16[3072,768]{1,0:T(8,128)(2,1)} fusion(bf16[1024,3072]{1,0:T(8,128)(2,1)} %copy-done.32, f32[1024,768]{1,0:T(8,128)S(1)} %copy-done.13), kind=kOutput, calls=%fused_computation.21 | convolution fusion | flops 4834983936 | bytes 14155776 | tf_op jit(solution)/shard_map/dot_general | solution.py:14
  485.9 6.8 copy.111
  492.6 3.6 copy.133
  496.2 3.1 copy.112
  501.9 38.8 %all-reduce.2 = (bf16[32,2,96]{2,1,0:T(2,128)(2,1)S(1)}, bf16[32,1,96]{2,0,1:T(8,128)(2,1)S(1)}) all-reduce(bf16[32,2,96]{2,1,0:T(2,128)(2,1)S(1)} %copy.114, bf16[32,1,96]{2,0,1:T(8,128)(2,1)S(1)} %bitcast.225), channel_id=12, replica_groups=mesh['rows'=8,'head'=4] {'rows','head'}, use_global_device_ids=true, to_apply=%region_19.20.clone | all-reduce | flops 9216 | bytes 36864
  541.8 10.1 %convolution_add_fusion = f32[1024,768]{1,0:T(8,128)} fusion(f32[1024,768]{1,0:T(8,128)} %copy-done.6, bf16[1024,2304]{0,1:T(8,128)(2,1)} %bitcast.207, bf16[768,2304]{1,0:T(8,128)(2,1)} %reshape.314), kind=kOutput, calls=%fused_computation.57 | convolution fusion | flops 3624665088 | bytes 14548992 | tf_op jit(solution)/shard_map/dot_general | solution.py:20
  553.3 22.8 %reduce-scatter.6.cloned.1.call-done = bf16[1,96,576]{2,1,0:T(8,128)(2,1)} async-done(((bf16[32,96,576]{2,1,0:T(8,128)(2,1)}), bf16[1,96,576]{2,1,0:T(8,128)(2,1)}) %reduce-scatter.6.cloned.1.call-update) | async-done | bytes 110608 | tf_op jit(solution)/shard_map/reduce_scatter | solution.py:102
  576.1 1.6 bitcast_convert_fusion.2
  577.7 110.7 %reduce-scatter.10.cloned.1.call-done = bf16[1,96,768]{2,1,0:T(8,128)(2,1)} async-done(((bf16[32,96,768]{2,1,0:T(8,128)(2,1)}), bf16[1,96,768]{2,1,0:T(8,128)(2,1)}) %reduce-scatter.10.cloned.1.call-update) | async-done | bytes 147472 | tf_op jit(solution)/shard_map/reduce_scatter | solution.py:102
  688.4 1.6 bitcast_convert_fusion.1
  690.0 110.6 %reduce-scatter.12.cloned.1.call-done = bf16[1,384,192]{1,2,0:T(8,128)(2,1)} async-done(((bf16[32,384,192]{1,2,0:T(8,128)(2,1)}), bf16[1,384,192]{1,2,0:T(8,128)(2,1)}) %reduce-scatter.12.cloned.1.call-update) | async-done | bytes 147472 | tf_op jit(solution)/shard_map/reduce_scatter | solution.py:102
  800.6 1.6 bitcast_convert_fusion
  (138 shorter events, 18.8 us)
Async XLA Ops:
  7.2 87.6 %all-gather.15.cloned.1.call-start = ((), (), s32[]{:S(2)}) async-start(), calls=%async_computation.9 | async-start | bytes 1622016 | tf_op jit(solution)/shard_map/all_gather | solution.py:88
  7.9 123.6 %all-gather.13.cloned.1.call-start = ((), (), s32[]{:S(2)}) async-start(), calls=%async_computation.8 | async-start | bytes 4055040 | tf_op jit(solution)/shard_map/all_gather | solution.py:88
  8.7 215.0 %all-gather.17.cloned.1.call-start = ((), (), s32[]{:S(2)}) async-start(), calls=%async_computation.10 | async-start | bytes 4866048 | tf_op jit(solution)/shard_map/all_gather | solution.py:88
  9.4 252.1 %all-gather.19.cloned.1.call-start = ((), (), s32[]{:S(2)}) async-start(), calls=%async_computation.11 | async-start | bytes 4866048 | tf_op jit(solution)/shard_map/all_gather | solution.py:88
  10.0 541.9 %reduce-scatter.8.cloned.1.call-start = ((), (), s32[]{:S(2)}) async-start(), calls=%async_computation.5 | async-start | bytes 1622016 | tf_op jit(solution)/shard_map/reduce_scatter | solution.py:102
  92.2 228.7 %copy-start.17 = (f32[768]{0:T(1024)}, f32[768]{0:T(1024)S(1)}, u32[]{:S(2)}) copy-start(f32[768]{0:T(1024)S(1)} %mul.161) | copy-start | bytes 9220
  92.3 193.4 %copy-start.25 = (f32[768]{0:T(1024)}, f32[768]{0:T(1024)S(1)}, u32[]{:S(2)}) copy-start(f32[768]{0:T(1024)S(1)} %add.130) | copy-start | bytes 9220
  137.5 8.0 copy-start.29
  173.4 10.9 %copy-start.2 = (bf16[2,512,12,1,64]{1,0,4,3,2:T(2,128)(2,1)}, bf16[2,512,12,1,64]{1,0,4,3,2:T(2,128)(2,1)S(1)}, u32[]{:S(2)}) copy-start(bf16[2,512,12,1,64]{1,0,4,3,2:T(2,128)(2,1)S(1)} %get-tuple-element.64) | copy-start | bytes 4718596
  173.4 10.9 %copy-start.4 = (bf16[2,512,12,1,64]{1,0,4,3,2:T(2,128)(2,1)}, bf16[2,512,12,1,64]{1,0,4,3,2:T(2,128)(2,1)S(1)}, u32[]{:S(2)}) copy-start(bf16[2,512,12,1,64]{1,0,4,3,2:T(2,128)(2,1)S(1)} %get-tuple-element.63) | copy-start | bytes 4718596
  217.7 2.1 copy-start.30
  219.7 1.6 copy-start.15
  221.4 1.7 copy-start.7
  223.6 97.4 %copy-start.19 = (f32[1024]{0:T(1024)}, f32[1024]{0:T(1024)S(1)}, u32[]{:S(2)}) copy-start(f32[1024]{0:T(1024)S(1)} %add_rsqrt_fusion.1) | copy-start | bytes 12292
  272.6 1.9 copy-start.8
  272.6 3.3 copy-start.11
  285.6 5.5 copy-start.32
  291.1 1.4 copy-start
  297.2 14.9 %copy-start.12 = (f32[1024,768]{1,0:T(8,128)}, f32[1024,768]{1,0:T(8,128)S(1)}, u32[]{:S(2)}) copy-start(f32[1024,768]{1,0:T(8,128)S(1)} %get-tuple-element.57) | copy-start | bytes 9437188
  322.8 2.6 copy-start.6
  363.7 2.7 copy-start.16
  370.8 205.3 %reduce-scatter.6.cloned.1.call-start = ((), (), s32[]{:S(2)}) async-start(), calls=%async_computation.4 | async-start | bytes 4055040 | tf_op jit(solution)/shard_map/reduce_scatter | solution.py:102
  370.8 21.9 %copy-start.5 = (bf16[2,512,12,1,64]{1,0,4,3,2:T(2,128)(2,1)S(1)}, bf16[2,512,12,1,64]{1,0,4,3,2:T(2,128)(2,1)}, u32[]{:S(2)}) copy-start(bf16[2,512,12,1,64]{1,0,4,3,2:T(2,128)(2,1)} %copy-done.4) | copy-start | bytes 4718596
  392.8 8.7 %copy-start.3 = (bf16[2,512,12,1,64]{1,0,4,3,2:T(2,128)(2,1)S(1)}, bf16[2,512,12,1,64]{1,0,4,3,2:T(2,128)(2,1)}, u32[]{:S(2)}) copy-start(bf16[2,512,12,1,64]{1,0,4,3,2:T(2,128)(2,1)} %copy-done.2) | copy-start | bytes 4718596
  401.5 7.0 copy-start.14
  420.5 6.1 copy-start.31
  424.4 2.1 copy-start.10
  447.0 1.9 copy-start.9
  447.0 1.9 copy-start.18
  447.0 1.9 copy-start.20
  447.0 1.9 copy-start.26
  447.0 241.4 %reduce-scatter.10.cloned.1.call-start = ((), (), s32[]{:S(2)}) async-start(), calls=%async_computation.6 | async-start | bytes 4866048 | tf_op jit(solution)/shard_map/reduce_scatter | solution.py:102
  474.0 1.9 copy-start.13
  474.0 326.7 %reduce-scatter.12.cloned.1.call-start = ((), (), s32[]{:S(2)}) async-start(), calls=%async_computation.7 | async-start | bytes 4866048 | tf_op jit(solution)/shard_map/reduce_scatter | solution.py:102
  499.4 1.4 copy-start.1
  499.4 1.8 copy-start.22
  499.4 1.9 copy-start.24
  499.4 1.9 copy-start.28
  499.4 2.0 copy-start.21
  499.4 2.0 copy-start.27
  499.4 2.1 copy-start.23
Sparse Core Ops, SparseCore 0:
  10.9 57.6 all-gather.14
  71.5 59.9 all-gather.12
  134.4 62.3 all-gather.16
  199.6 61.8 all-gather.18
  370.9 96.0 reduce-scatter.7
  472.3 103.7 reduce-scatter.5
  581.6 106.7 reduce-scatter.9
  693.9 106.7 reduce-scatter.11

commit v2 on v1

--- a/solution.py
+++ b/solution.py
@@ -1,6 +1,10 @@
+import functools
+
 import jax
 import jax.numpy as jnp
 from jax import lax
+from jax.experimental import pallas as pl
+from jax.experimental.pallas import tpu as pltpu
 from jax.sharding import PartitionSpec as P
 
 HD = 64
@@ -102,7 +106,7 @@
     return lax.psum_scatter(parts, AXES, scatter_dimension=0, tiled=False).astype(jnp.float32)
 
 
-def shards(
+def shards_plain(
     inputs,
     qkv_weight,
     out_weight,
@@ -194,13 +198,492 @@
     )
 
 
+MESH = pl.DeviceIdType.MESH
+NZ, NX, NY, NC = 4, 2, 2, 2
+FIRST = ("x", "x", "y", "y", "x")
+
+
+def spot():
+    r, h = lax.axis_index("rows"), lax.axis_index("head")
+    return r // NX, lax.rem(r, NX), h // NC, lax.rem(h, NC)
+
+
+def dev(z, x, y, c):
+    return (z * NX + x, y * NC + c)
+
+
+def other_z(z, d):
+    return lax.rem(z + d, NZ)
+
+
+def meet(z, x, y, c):
+    barrier = pltpu.get_barrier_semaphore()
+    mates = [dev(other_z(z, d), x, y, c) for d in range(1, NZ)]
+    mates += [dev(z, 1 - x, y, c), dev(z, x, 1 - y, c), dev(z, x, y, 1 - c)]
+    for mate in mates:
+        pl.semaphore_signal(barrier, inc=1, device_id=mate, device_id_type=MESH)
+    pl.semaphore_wait(barrier, len(mates))
+
+
+def tile(w, ref, z, x, y, c):
+    r, h = dev(z, x, y, c)
+    if w == 2:
+        return ref.at[pl.ds(pl.multiple_of(r * 96, 32), 96), pl.ds(pl.multiple_of(h * 768, 128), 768)]
+    if w == 3:
+        return ref.at[pl.ds(pl.multiple_of(h * 192, 64), 192), pl.ds(pl.multiple_of(r * 384, 128), 384)]
+    return ref.at[h, r]
+
+
+class Spread:
+    def __init__(self, ins, outs, send_sem, recv_sem, local_sem):
+        self.ins, self.outs = ins, outs
+        self.send_sem, self.recv_sem, self.local_sem = send_sem, recv_sem, local_sem
+        self.at = spot()
+        self.sent = {w: [] for w in range(5)}
+        self.locals = []
+
+    def push(self, w, src, shard, to):
+        k = len(self.sent[w])
+        copy = pltpu.make_async_remote_copy(
+            src_ref=src,
+            dst_ref=tile(w, self.outs[w], *shard),
+            send_sem=self.send_sem.at[w, k],
+            recv_sem=self.recv_sem.at[w, self.index(shard)],
+            device_id=to,
+            device_id_type=MESH,
+        )
+        copy.start()
+        self.sent[w].append(copy)
+
+    def index(self, shard):
+        r, h = dev(*shard)
+        return r * (NY * NC) + h
+
+    def take(self, w, shard):
+        there = tile(w, self.outs[w], *shard)
+        pltpu.make_async_remote_copy(
+            src_ref=there,
+            dst_ref=there,
+            send_sem=self.send_sem.at[w, 0],
+            recv_sem=self.recv_sem.at[w, self.index(shard)],
+            device_id=dev(self.at[0], self.at[1], self.at[2], 1 - self.at[3]),
+            device_id_type=MESH,
+        ).wait_recv()
+
+    def spread(self, w, src, shard, kinds):
+        z, x, y, c = self.at
+        to = {"x": dev(z, 1 - x, y, c), "y": dev(z, x, 1 - y, c), "c": dev(z, x, y, 1 - c)}
+        for kind in kinds:
+            self.push(w, src, shard, to[kind])
+
+    def open(self, w):
+        z, x, y, c = self.at
+        src = self.ins[w]
+        for d in range(1, NZ):
+            self.push(w, src, self.at, dev(other_z(z, d), x, y, c))
+        second = "y" if FIRST[w] == "x" else "x"
+        self.spread(w, src, self.at, (FIRST[w], second, "c"))
+        local = pltpu.make_async_copy(src, tile(w, self.outs[w], *self.at), self.local_sem.at[w])
+        local.start()
+        self.locals.append(local)
+
+    def near(self, w):
+        z, x, y, c = self.at
+        second = "y" if FIRST[w] == "x" else "x"
+        for d in range(1, NZ):
+            shard = (other_z(z, d), x, y, c)
+            self.take(w, shard)
+            self.spread(w, tile(w, self.outs[w], *shard), shard, (FIRST[w], second, "c"))
+
+    def middle(self, w):
+        z, x, y, c = self.at
+        second = "y" if FIRST[w] == "x" else "x"
+        for d in range(NZ):
+            shard = (other_z(z, d), 1 - x, y, c) if FIRST[w] == "x" else (other_z(z, d), x, 1 - y, c)
+            self.take(w, shard)
+            self.spread(w, tile(w, self.outs[w], *shard), shard, (second, "c"))
+
+    def far(self, w):
+        z, x, y, c = self.at
+        for e in range(2):
+            for d in range(NZ):
+                if FIRST[w] == "x":
+                    shard = (other_z(z, d), x if e == 0 else 1 - x, 1 - y, c)
+                else:
+                    shard = (other_z(z, d), 1 - x, y if e == 0 else 1 - y, c)
+                self.take(w, shard)
+                self.spread(w, tile(w, self.outs[w], *shard), shard, ("c",))
+
+    def core(self, w):
+        z, x, y, c = self.at
+        for ey in range(2):
+            for ex in range(2):
+                for d in range(NZ):
+                    self.take(
+                        w,
+                        (other_z(z, d), x if ex == 0 else 1 - x, y if ey == 0 else 1 - y, 1 - c),
+                    )
+
+    def close(self):
+        for local in self.locals:
+            local.wait()
+        for copies in self.sent.values():
+            for copy in copies:
+                copy.wait_send()
+
+
+def gather_kernel(*refs):
+    ins, outs = refs[:5], refs[5:10]
+    s = Spread(ins, outs, *refs[10:])
+    meet(*s.at)
+    s.open(0)
+    s.open(4)
+    s.near(0)
+    for w in (1, 2, 3):
+        s.open(w)
+    s.near(4)
+    s.middle(0)
+    s.near(1)
+    s.middle(4)
+    s.near(2)
+    s.far(0)
+    s.far(4)
+    s.middle(1)
+    s.near(3)
+    s.middle(2)
+    s.far(1)
+    s.middle(3)
+    s.far(2)
+    s.far(3)
+    for w in range(5):
+        s.core(w)
+    s.close()
+
+
+GATHERED = ((4, 8, 96, 576), (4, 8, 96, 192), (768, 3072), (768, 3072), (4, 8, 8, 128))
+
+
+def gather_all(qkv, out, up, down_t, small):
+    return pl.pallas_call(
+        gather_kernel,
+        out_shape=[
+            jax.ShapeDtypeStruct(shape, jnp.float32 if i == 4 else jnp.bfloat16)
+            for i, shape in enumerate(GATHERED)
+        ],
+        in_specs=[pl.BlockSpec(memory_space=pltpu.VMEM)] * 5,
+        out_specs=[pl.BlockSpec(memory_space=pl.ANY)] * 5,
+        scratch_shapes=[
+            pltpu.SemaphoreType.DMA((5, 31)),
+            pltpu.SemaphoreType.DMA((5, 32)),
+            pltpu.SemaphoreType.DMA((5,)),
+        ],
+        compiler_params=pltpu.CompilerParams(collective_id=0, has_side_effects=True),
+        name="gather_weights",
+    )(qkv, out, up, down_t, small)
+
+
+SHARD = ((96, 576), (96, 192), (96, 768), (192, 384), (8, 128))
+
+
+def kind_of(w):
+    return jnp.float32 if w == 4 else jnp.bfloat16
+
+
+class Reduce:
+    def __init__(self, acc, from_core, from_second, from_first, from_z, send_sem, recv_sem):
+        self.acc = acc
+        self.slots = (from_core, from_second, from_first, from_z)
+        self.send_sem, self.recv_sem = send_sem, recv_sem
+        self.at = spot()
+
+    def shard(self, w, d, e1, e2, ec):
+        z, x, y, c = self.at
+        flip = lambda v, e: v + e * (1 - 2 * v)
+        ex, ey = (e1, e2) if FIRST[w] == "x" else (e2, e1)
+        return (other_z(z, d), flip(x, ex), flip(y, ey), flip(c, ec))
+
+    def order(self, stage, k):
+        if stage == 0:
+            return (lax.rem(k, 4), 1 - lax.rem(k // 4, 2), 1 - k // 8)
+        if stage == 1:
+            return (lax.rem(k, 4), 1 - k // 4, 0)
+        return (lax.rem(k + 1, 4), 0, 0)
+
+    def slot(self, w, stage, shard):
+        z, x, y, c = shard
+        first, second = (x, y) if FIRST[w] == "x" else (y, x)
+        if stage == 0:
+            return (z * 2 + first) * 2 + second
+        if stage == 1:
+            return z * 2 + first
+        return z
+
+    def sending(self, w, stage, k):
+        z, x, y, c = self.at
+        if stage == 0:
+            shard = self.shard(w, lax.rem(k, 4), 1 - lax.rem(k // 4, 2), 1 - k // 8, 1)
+            to, place, base = dev(z, x, y, 1 - c), self.slot(w, 0, shard), 0
+        elif stage == 1:
+            shard = self.shard(w, lax.rem(k, 4), 1 - k // 4, 1, 0)
+            to = dev(z, x, 1 - y, c) if FIRST[w] == "x" else dev(z, 1 - x, y, c)
+            place, base = self.slot(w, 1, shard), 16
+        elif stage == 2:
+            shard = self.shard(w, lax.rem(k + 1, 4), 1, 0, 0)
+            to = dev(z, 1 - x, y, c) if FIRST[w] == "x" else dev(z, x, 1 - y, c)
+            place, base = self.slot(w, 2, shard), 24
+        else:
+            shard = self.shard(w, k + 1, 0, 0, 0)
+            to, place, base = dev(other_z(z, k + 1), x, y, c), k, 28
+        return pltpu.make_async_remote_copy(
+            src_ref=tile(w, self.acc[w], *shard),
+            dst_ref=self.slots[stage][w].at[place],
+            send_sem=self.send_sem.at[w, base + k],
+            recv_sem=self.recv_sem.at[w, base + place],
+            device_id=to,
+            device_id_type=MESH,
+        )
+
+    def arrive(self, w, stage, place):
+        z, x, y, c = self.at
+        here = self.slots[stage][w].at[place]
+        base = (0, 16, 24, 28)[stage]
+        pltpu.make_async_remote_copy(
+            src_ref=here,
+            dst_ref=here,
+            send_sem=self.send_sem.at[w, base],
+            recv_sem=self.recv_sem.at[w, base + place],
+            device_id=dev(z, x, y, 1 - c),
+            device_id_type=MESH,
+        ).wait_recv()
+
+    def open(self, w):
+        def step(k, carry):
+            self.sending(w, 0, k).start()
+            return carry
+
+        lax.fori_loop(0, 16, step, 0)
+
+    def fold(self, w, stage):
+        count = (16, 8, 4)[stage]
+        leave = (8, 4, 3)[stage]
+
+        def step(k, carry):
+            d, e1, e2 = self.order(stage, k)
+            shard = self.shard(w, d, e1, e2, 0)
+            place = self.slot(w, stage, shard)
+            self.arrive(w, stage, place)
+            mine = tile(w, self.acc[w], *shard)
+            total = mine[...].astype(jnp.float32) + self.slots[stage][w][place].astype(jnp.float32)
+            mine[...] = total.astype(kind_of(w))
+
+            @pl.when(jnp.logical_and(k >= 1, k <= leave))
+            def _():
+                self.sending(w, stage + 1, k - 1).start()
+
+            return carry
+
+        lax.fori_loop(0, count, step, 0)
+
+    def finish(self, w, out):
+        total = tile(w, self.acc[w], *self.at)[...].astype(jnp.float32)
+        for k in range(3):
+            self.arrive(w, 3, k)
+            total = total + self.slots[3][w][k].astype(jnp.float32)
+        out[...] = total
+
+    def close(self, w):
+        for stage, count in enumerate((16, 8, 4, 3)):
+
+            def step(k, carry, stage=stage):
+                self.sending(w, stage, k).wait_send()
+                return carry
+
+            lax.fori_loop(0, count, step, 0)
+
+
+def reduce_scratch():
+    scratch = []
+    for count in (16, 8, 4, 3):
+        scratch += [pltpu.VMEM((count,) + SHARD[w], kind_of(w)) for w in range(5)]
+    return scratch
+
+
+def scatter_kernel(*refs):
+    ins, outs, acc = refs[:5], refs[5:10], refs[10:15]
+    slots = [refs[15 + 5 * i : 20 + 5 * i] for i in range(4)]
+    send_sem, recv_sem, local_sem = refs[35:]
+    s = Reduce(acc, *slots, send_sem, recv_sem)
+    loads = [pltpu.make_async_copy(ins[w], acc[w], local_sem.at[w]) for w in range(5)]
+    waves = (3, 2, 0, 1, 4)
+    for w in waves:
+        loads[w].start()
+    meet(*s.at)
+    for i in range(len(waves) + 3):
+        if i < len(waves):
+            loads[waves[i]].wait()
+            s.open(waves[i])
+        for stage in range(3):
+            j = i - stage
+            if 0 <= j < len(waves):
+                s.fold(waves[j], stage)
+        j = i - 3
+        if 0 <= j < len(waves):
+            s.finish(waves[j], outs[waves[j]])
+    for w in waves:
+        s.close(w)
+
+
+def scatter_all(*grads):
+    return pl.pallas_call(
+        scatter_kernel,
+        out_shape=[jax.ShapeDtypeStruct(shape, jnp.float32) for shape in SHARD],
+        in_specs=[pl.BlockSpec(memory_space=pl.ANY)] * 5,
+        out_specs=[pl.BlockSpec(memory_space=pltpu.VMEM)] * 5,
+        scratch_shapes=[pltpu.VMEM(GATHERED[w], kind_of(w)) for w in range(5)]
+        + reduce_scratch()
+        + [
+            pltpu.SemaphoreType.DMA((5, 31)),
+            pltpu.SemaphoreType.DMA((5, 31)),
+            pltpu.SemaphoreType.DMA((5,)),
+        ],
+        compiler_params=pltpu.CompilerParams(
+            collective_id=1, has_side_effects=True, vmem_limit_bytes=60 * 1024 * 1024
+        ),
+        name="scatter_grads",
+    )(*grads)
+
+
+def fits(mesh):
+    return dict(mesh.shape) == {"rows": NZ * NX, "head": NY * NC}
+
+
+def shards(*args, fast):
+    return shards_fast(*args) if fast else shards_plain(*args)
+
+
+def shards_fast(
+    inputs,
+    qkv_weight,
+    out_weight,
+    up_weight,
+    down_weight,
+    biases,
+    norm_params,
+    cotangent,
+    boundaries,
+    lengths,
+):
+    micro, seq_per, seq, width = inputs.shape
+    count = micro * seq_per
+    heads = width // HD
+    groups = NY * NC
+    small = jnp.concatenate([biases, norm_params], axis=0).astype(jnp.float32)
+    small = jnp.pad(small, ((0, 5), (0, 32)))
+    qkv_full, out_full, up_full, down_t, small_full = gather_all(
+        qkv_weight, out_weight, up_weight, down_weight.T, small
+    )
+    qkv_full = qkv_full.reshape(groups, width, -1)
+    out_full = out_full.reshape(groups, width, -1)
+    bias_float = small_full[:, :, :2, :96].transpose(0, 2, 1, 3).reshape(8, width)
+    norm_float = small_full[:, :, 2, :96].reshape(4, width)
+    first_seq = lax.axis_index("head") * seq_per
+    bounds = lax.dynamic_slice_in_dim(boundaries, first_seq, seq_per, 1).reshape(count)
+    lens = lax.dynamic_slice_in_dim(lengths, first_seq, seq_per, 1).reshape(count)
+
+    tokens = inputs.reshape(count * seq, width)
+    zero_part = jnp.zeros((heads, HD), jnp.float32)
+    head_bias = jnp.stack(
+        [bias_float[0].reshape(heads, HD), zero_part, bias_float[1].reshape(heads, HD)], axis=1
+    ).reshape(3 * width)
+    project = jnp.einsum("td,gde->tge", tokens, qkv_full, preferred_element_type=jnp.float32)
+    project = (project.reshape(-1, 3 * width) + head_bias).astype(jnp.bfloat16)
+    items = project.reshape(count, seq, heads, 3, HD)
+    q, k, v = items[:, :, :, 0], items[:, :, :, 1], items[:, :, :, 2]
+    context, log_total = jax.vmap(attend_forward)(q, k, v, bounds, lens)
+    context = context.reshape(count * seq, width)
+    attended = jnp.einsum("td,gde->tge", context, out_full, preferred_element_type=jnp.float32)
+    attended = attended.reshape(-1, width) + bias_float[2]
+    hidden, normed_one, scale_one = norm_forward(
+        tokens.astype(jnp.float32) + attended, norm_float[0], norm_float[1]
+    )
+    hidden_low = hidden.astype(jnp.bfloat16)
+    inner_pre = jnp.dot(hidden_low, up_full, preferred_element_type=jnp.float32) + bias_float[
+        4:8
+    ].reshape(-1)
+    cdf = 0.5 * (1.0 + lax.erf(inner_pre * ROOT_HALF))
+    active_low = (inner_pre * cdf).astype(jnp.bfloat16)
+    slope = cdf + inner_pre * jnp.exp(-0.5 * inner_pre * inner_pre) * INVERSE_ROOT_TWO_PI
+    outer_out = contract_cols(active_low, down_t) + bias_float[3]
+    output_float, normed_two, scale_two = norm_forward(
+        hidden + outer_out, norm_float[2], norm_float[3]
+    )
+    grad_out = cotangent.reshape(count * seq, width).astype(jnp.float32)
+    grad_two, gain_two, shift_two = norm_backward(grad_out, normed_two, scale_two, norm_float[2])
+    grad_two_low = grad_two.astype(jnp.bfloat16)
+    down_grad = contract_rows(grad_two_low, active_low).astype(jnp.bfloat16)
+    grad_inner = jnp.dot(grad_two_low, down_t, preferred_element_type=jnp.float32) * slope
+    grad_inner_low = grad_inner.astype(jnp.bfloat16)
+    up_grad = contract_rows(hidden_low, grad_inner_low).astype(jnp.bfloat16)
+    grad_hidden = contract_cols(grad_inner_low, up_full) + grad_two
+    grad_one, gain_one, shift_one = norm_backward(grad_hidden, normed_one, scale_one, norm_float[0])
+    grad_one_low = grad_one.astype(jnp.bfloat16)
+    grad_one_parts = grad_one_low.reshape(-1, groups, width // groups)
+    out_grad = jnp.einsum(
+        "td,tge->gde", context, grad_one_parts, preferred_element_type=jnp.float32
+    ).astype(jnp.bfloat16).reshape(GATHERED[1])
+    grad_context = jnp.einsum(
+        "tge,gde->td", grad_one_parts, out_full, preferred_element_type=jnp.float32
+    ).astype(jnp.bfloat16)
+    grad_items = grad_context.reshape(count, seq, heads, HD)
+    grad_project = jax.vmap(attend_backward)(q, k, v, bounds, lens, log_total, grad_items)
+    grad_project = grad_project.reshape(count * seq, 3 * width)
+    parts = grad_project.reshape(count * seq, groups, -1)
+    qkv_grad = jnp.einsum(
+        "td,tge->gde", tokens, parts, preferred_element_type=jnp.float32
+    ).astype(jnp.bfloat16).reshape(GATHERED[0])
+    grad_input = (
+        jnp.einsum("tge,gde->td", parts, qkv_full, preferred_element_type=jnp.float32) + grad_one
+    )
+    project_sums = jnp.sum(grad_project, axis=0, dtype=jnp.float32).reshape(heads, 3, HD)
+    bias_grad = jnp.concatenate(
+        [
+            project_sums[:, 0].reshape(1, width),
+            project_sums[:, 2].reshape(1, width),
+            jnp.sum(grad_one, axis=0).reshape(1, width),
+            jnp.sum(grad_two, axis=0).reshape(1, width),
+            jnp.sum(grad_inner, axis=0).reshape(4, width),
+        ],
+        axis=0,
+    )
+    norm_grad = jnp.stack([gain_one, shift_one, gain_two, shift_two])
+    small_grad = jnp.concatenate(
+        [
+            bias_grad.reshape(groups, 2, 8, 96).transpose(0, 2, 1, 3),
+            norm_grad.reshape(groups, 1, 8, 96).transpose(0, 2, 1, 3),
+        ],
+        axis=2,
+    )
+    small_grad = jnp.pad(small_grad, ((0, 0), (0, 0), (0, 5), (0, 32)))
+    own = scatter_all(qkv_grad, out_grad, up_grad, down_grad, small_grad)
+    return (
+        output_float.astype(jnp.bfloat16).reshape(inputs.shape),
+        grad_input.reshape(inputs.shape),
+        own[0],
+        own[1],
+        own[2],
+        own[3].T,
+        own[4][:2, :96],
+        own[4][2:3, :96],
+    )
+
+
 def solution(mesh):
     tokens = P(None, ("rows", "head"), None, None)
     weight = P("rows", "head")
     small = P("head", "rows")
     per_row = P(None, "rows")
     return jax.shard_map(
-        shards,
+        functools.partial(shards, fast=fits(mesh)),
         mesh=mesh,
         in_specs=(tokens, weight, weight, weight, weight, small, small, tokens, per_row, per_row),
         out_specs=(tokens, tokens, weight, weight, weight, weight, small, small),

time: 821 us -> 475 us (0.58)
  waiting for transfers between devices: 309 us -> 0 us
  Pallas kernels: 0 us -> 195 us
  blocking collectives: 119 us -> 0 us
  local copies, waits for them, and re-layouts: 142 us -> 65.8 us
  matrix products: 170 us -> 147 us
  between operations: 14.8 us -> 1.64 us
    reduce_scatter x4 -> x0, waiting for transfers between devices: 244 us -> none  [scatter(): lax.psum_scatter(parts, AXES, scatter_dimension=0, tiled=False)]
    pallas_call x0 -> x2, Pallas kernels: none -> 195 us  [the longest x1 108 us: scatter_all(): pl.pallas_call(scatter_kernel, out_shape=[jax.ShapeDtypeStruct(shape, jnp...]
    all_gather x2 -> x0, blocking collectives: 80.3 us -> none  [gather(): lax.all_gather(shard, AXES, axis=0, tiled=False).reshape(rows, head, a, b)]
    all_gather x4 -> x0, waiting for transfers between devices: 62.1 us -> none  [gather(): lax.all_gather(shard, AXES, axis=0, tiled=False).reshape(rows, head, a, b)]
    unnamed x1 -> x0, blocking collectives: 38.8 us -> none
    reshape x12 -> x9, local copies, waits for them, and re-layouts: 47.2 us -> 17 us  [the longest x1 13.2 us: shards_fast(): project = (project.reshape(-1, 3 * width) + head_bias).astype(jnp.bfloat16)]
    dot_general x4 -> x8, matrix products: 24.3 us -> 51.7 us  [the longest x1 12 us: shards_fast(): jnp.dot(grad_two_low, down_t, preferred_element_type=jnp.float32) * slope]
    dot_general x4 -> x2, matrix products: 36.4 us -> 13 us  [contract_cols(): lax.dot_general(left, right, (((1,), (1,)), ((), ())), preferred_element_...]
  transfers between devices with their start and end apart: 8 -> 0, of which waited for: 5 -> 0; matrix products, arithmetic and copies ran while one was open for 30% -> 0% of each run, Pallas kernels for 0% -> 0%
where the time goes in v2:
time: 475 us; the launch traced here: 466 us
  Pallas kernels  195 us (41%)
  matrix products  147 us (31%)
  local copies, waits for them, and re-layouts  65.8 us (14%)
  other arithmetic  56 us (12%)
    pallas_call x1, Pallas kernels, scatter_all(): pl.pallas_call(scatter_kernel, out_shape=[jax.ShapeDtypeStruct(shape, jnp...  108 us
    pallas_call x1, Pallas kernels, gather_all(): pl.pallas_call(gather_kernel, out_shape=[jax.ShapeDtypeStruct(shape, jnp....  87 us
    convert_element_type x1, other arithmetic, attend_backward(): (weights_full * (grad_weights - inner_sum)).astype(jnp.bfloat16)  21.7 us
    convert_element_type x2, local copies, waits for them, and re-layouts, attend_backward(): jnp.stack([grad_queries, grad_keys, grad_values], axis=2)  18.5 us
    dot_general x1, matrix products, attend_backward(): jnp.einsum('qhe,khe->hqk', grad_context, values_in, preferred_element_typ...  17.2 us
    dot_general x2, matrix products, contract_rows(): lax.dot_general(left, right, (((0,), (0,)), ((), ())), preferred_element_...  15.2 us
    reshape x1, local copies, waits for them, and re-layouts, shards_fast(): project = (project.reshape(-1, 3 * width) + head_bias).astype(jnp.bfloat16)  13.2 us
    dot_general x2, matrix products, contract_cols(): lax.dot_general(left, right, (((1,), (1,)), ((), ())), preferred_element_...  13 us

profile of v2, /device:TPU:0, one launch (start us, length us, event | category | flops | bytes accessed | tf_op | source)
XLA Modules:
  0.0 465.9 jit_solution(3547818831016485709)
XLA Ops:
  0.7 0.9 dynamic-slice_reduce_fusion
  1.8 1.3 fusion.64.refs_4_
  3.0 0.5 compare_and_fusion
  3.6 87.0 %gather_weights.1 = (bf16[4,8,96,576]{3,2,1,0:T(8,128)(2,1)}, bf16[4,8,96,192]{3,2,1,0:T(8,128)(2,1)}, bf16[768,3072]{1,0:T(8,128)(2,1)}, bf16[768,3072]{1,0:T(8,128)(2,1)}, f32[4,8,8,128]{3,2,1,0:T(8,128)}) custom-call(bf16[96,576]{1,0:T(8,128)(2,1)} %refs_0_.1, bf16[96,192]{1,0:T(8,128)(2,1)} %refs_1_.1, bf16[96,768]{1,0:T(8,128)(2,1)} %refs_2_.1, ...), custom_call_target="tpu_custom_call" | custom-call | tf_op jit(solution)/shard_map/gather_weights/pallas_call | solution.py:367
  90.6 1.0 slice_reduce_fusion.1
  91.6 0.9 slice_bitcast_fusion.9
  92.8 2.1 convert_reduce_fusion.1
  94.9 0.7 stack.38
  96.0 0.7 copy.62
  96.7 10.6 %convolution_bitcast_fusion = f32[1024,4,576]{0,2,1:T(8,128)} fusion(bf16[4,768,576]{2,1,0:T(8,128)(2,1)} %bitcast.156, bf16[1024,768,1]{1,0,2:T(8,128)(2,1)} %bitcast.158), kind=kOutput, calls=%fused_computation.27 | convolution fusion | flops 3623878656 | bytes 14548992 | tf_op jit(solution)/shard_map/td,gde->tge/dot_general | solution.py:598
  107.3 13.2 %reshape.241 = f32[2,512,12,3,64]{1,0,4,3,2:T(2,128)} reshape(f32[1024,4,576]{0,2,1:T(8,128)} %convolution_bitcast_fusion) | data formatting | bytes 18874368 | tf_op jit(solution)/shard_map/reshape | solution.py:599
  120.6 5.2 %fusion.11 = bf16[2,512,12,3,64]{1,4,2,0,3:T(8,128)(2,1)S(1)} fusion(f32[2,512,12,3,64]{1,0,4,3,2:T(2,128)} %reshape.241, f32[12,3,64]{2,0,1:T(8,128)S(1)} %pad_maximum_fusion), kind=kLoop, calls=%fused_computation.21 | loop fusion | flops 4718592 | bytes 14164992 | tf_op jit(solution)/shard_map/convert_element_type | solution.py:599
  125.8 10.5 %fusion.12 = (f32[2,12,512]{2,1,0:T(8,128)S(1)}, f32[2,12,512,512]{2,3,1,0:T(8,128)}) fusion(pred[2,512,512]{1,2,0:T(8,128)(4,1)S(1)} %compare_and_fusion, bf16[2,512,12,3,64]{1,4,2,0,3:T(8,128)(2,1)S(1)} %fusion.11), kind=kOutput, calls=%fused_computation.23 | convolution fusion | flops 824168448 | bytes 28884992 | tf_op jit(solution)/shard_map/vmap(qhe,khe->hqk)/dot_general | solution.py:51
  136.3 11.0 %fusion = f32[2,12,512]{2,1,0:T(8,128)S(1)} fusion(f32[2,12,512]{2,1,0:T(8,128)S(1)} %get-tuple-element.77, f32[2,12,512,512]{2,3,1,0:T(8,128)} %get-tuple-element.78, pred[2,512,512]{1,2,0:T(8,128)(4,1)S(1)} %compare_and_fusion), kind=kLoop, calls=%fused_computation.6 | loop fusion | flops 25153536 | bytes 25788416 | tf_op jit(solution)/shard_map/vmap()/reduce_sum | solution.py:61
  147.4 12.0 %fusion.36 = bf16[2,512,12,64]{1,3,2,0:T(8,128)(2,1)S(1)} fusion(f32[2,12,512]{2,1,0:T(8,128)S(1)} %fusion, f32[2,12,512]{2,1,0:T(8,128)S(1)} %get-tuple-element.77, f32[2,12,512,512]{2,3,1,0:T(8,128)} %get-tuple-element.78, pred[2,512,512]{1,2,0:T(8,128)(4,1)S(1)} %compare_and_fusion, bf16[2,512,12,3,64]{1,4,2,0,3:T(8,128)(2,1)S(1)} %fusion.11), kind=kOutput, calls=%fused_computation.69 | convolution fusion | flops 837550080 | bytes 28966912 | tf_op jit(solution)/shard_map/vmap(hqk,khe->qhe)/dot_general | solution.py:63
  159.4 1.6 copy.61
  161.0 0.4 copy.89
  161.4 1.6 fusion.76
  163.1 0.5 multiply_reduce_fusion.4
  163.6 0.9 slice-done.2
  164.6 0.5 slice-done.3
  165.1 9.4 %multiply_convert_fusion.1 = (bf16[1024,3072]{1,0:T(8,128)(2,1)S(1)}, f32[1024,3072]{1,0:T(8,128)}) fusion(f32[3072]{0:T(1024)S(1)} %add.123, bf16[768,3072]{1,0:T(8,128)(2,1)S(1)} %bitcast.151, f32[1024,768]{1,0:T(8,128)S(1)} %get-tuple-element.80, f32[768]{0:T(1024)S(1)} %add.120, f32[768]{0:T(1024)S(1)} %mul.161, f32[1024]{0:T(1024)S(1)} %add_rsqrt_fusion.1, ...), kind=kOutput, calls=%fused_computation.16 | convolution fusion | flops 4854644736 | bytes 26765312 | tf_op jit(solution)/shard_map/dot_general | solution.py:610
  174.4 5.5 %fusion.77 = (f32[1024]{0:T(1024)S(1)}, f32[1024,768]{1,0:T(8,128)S(1)}) fusion(f32[768]{0:T(1024)S(1)} %get-tuple-element.64, bf16[1024,3072]{1,0:T(8,128)(2,1)S(1)} %get-tuple-element.81, bf16[768,3072]{1,0:T(8,128)(2,1)S(1)} %bitcast.155, f32[768]{0:T(1024)S(1)} %add.120, f32[768]{0:T(1024)S(1)} %mul.161, f32[1024]{0:T(1024)S(1)} %add_rsqrt_fusion.1, ...), kind=kOutput, calls=%fused_computation.134 | convolution fusion | flops 4837342208 | bytes 17323008 | tf_op jit(solution)/shard_map/dot_general | solution.py:24
  180.0 0.5 multiply_reduce_fusion.3
  180.5 0.9 copy-done.1
  181.3 1.2 fusion.19
  182.5 0.1 stack.37
  182.6 3.6 fusion.72
  186.2 12.0 %fusion.78 = (f32[3072]{0:T(1024)S(1)}, bf16[1024,3072]{1,0:T(8,128)(2,1)S(1)}) fusion(f32[1024,3072]{1,0:T(8,128)} %get-tuple-element.82, f32[3072]{0:T(1024)S(1)} %add.123, bf16[768,3072]{1,0:T(8,128)(2,1)} %get-tuple-element.22, f32[1024,768]{1,0:T(8,128)S(1)} %get-tuple-element.69), kind=kOutput, calls=%fused_computation.135 | convolution fusion | flops 4870370304 | bytes 26763264 | tf_op jit(solution)/shard_map/dot_general | solution.py:624
  198.3 7.3 %convolution_convert_fusion.refs_3_ = bf16[768,3072]{1,0:T(8,128)(2,1)} fusion(bf16[1024,3072]{1,0:T(8,128)(2,1)S(1)} %bitcast.163, f32[1024,768]{1,0:T(8,128)S(1)} %get-tuple-element.69), kind=kOutput, calls=%fused_computation.24 | convolution fusion | flops 4834983936 | bytes 14155776 | tf_op jit(solution)/shard_map/dot_general | solution.py:18
  205.6 7.5 %multiply_reduce_fusion.1 = (f32[768]{0:T(1024)S(1)}, f32[1024]{0:T(1024)S(1)}, f32[1024]{0:T(1024)S(1)}, f32[768]{0:T(1024)S(1)}, f32[1024,768]{1,0:T(8,128)}) fusion(f32[1024,768]{1,0:T(8,128)S(1)} %copy-done.7, f32[1024]{0:T(1024)S(1)} %add_rsqrt_fusion.1, f32[1024]{0:T(1024)S(1)} %broadcast_multiply_fusion.4, f32[768]{0:T(1024)S(1)} %mul.161, ...), kind=kOutput, calls=%fused_computation.41 | convolution fusion | flops 4839698432 | bytes 20472832 | tf_op jit(solution)/shard_map/dot_general | solution.py:24
  213.2 0.1 stack.35
  213.3 3.5 fusion.74
  216.8 0.2 copy-done.8
  217.0 1.9 copy-done.19
  218.9 7.9 %convolution_convert_fusion.1.refs_2_ = bf16[768,3072]{1,0:T(8,128)(2,1)} fusion(bf16[1024,3072]{1,0:T(8,128)(2,1)S(1)} %copy-done.19, f32[1024,768]{1,0:T(8,128)S(1)} %copy-done.8, f32[768]{0:T(1024)S(1)} %add.120, f32[768]{0:T(1024)S(1)} %mul.161, f32[1024]{0:T(1024)S(1)} %add_rsqrt_fusion.1, f32[1024]{0:T(1024)S(1)} %broadcast_multiply_fusion.4), kind=kOutput, calls=%fused_computation.25 | convolution fusion | flops 4838129664 | bytes 14170112 | tf_op jit(solution)/shard_map/dot_general | solution.py:18
  226.8 1.3 convert_element_type.109
  228.1 2.0 copy.64
  230.2 2.4 fusion.37
  232.6 1.9 bitcast_convert_fusion
  234.5 1.7 copy.66
  236.2 2.9 reshape.247
  239.1 2.5 copy.76
  241.7 12.7 %fusion.24 = bf16[2,512,12,1,64]{1,4,2,0,3:T(8,128)(2,1)} fusion(f32[2,12,512]{2,1,0:T(8,128)S(1)} %log_add_fusion, f32[2,12,512,512]{2,3,1,0:T(8,128)} %get-tuple-element.78, pred[2,512,512]{1,2,0:T(8,128)(4,1)S(1)} %copy-done.3, bf16[2,512,12,64]{1,0,3,2:T(2,128)(2,1)S(1)} %reshape.247), kind=kOutput, calls=%fused_computation.60 | convolution fusion | flops 830472192 | bytes 28884992 | tf_op jit(solution)/shard_map/vmap(hqk,qhe->khe)/dot_general | solution.py:72
  254.3 17.2 %multiply_reduce_fusion = (f32[2,12,512]{2,1,0:T(8,128)S(1)}, f32[2,12,512,512]{2,3,1,0:T(8,128)}) fusion(f32[2,12,512]{2,1,0:T(8,128)S(1)} %log_add_fusion, f32[2,12,512,512]{2,3,1,0:T(8,128)} %get-tuple-element.78, pred[2,512,512]{1,2,0:T(8,128)(4,1)S(1)} %copy-done.3, bf16[2,512,12,3,64]{1,4,2,0,3:T(8,128)(2,1)} %copy-done, ...), kind=kOutput, calls=%fused_computation.1 | convolution fusion | flops 836751360 | bytes 54099968 | tf_op jit(solution)/shard_map/vmap(qhe,khe->hqk)/dot_general | solution.py:75
  271.5 21.7 %multiply_convert_fusion = bf16[2,12,512,512]{2,3,1,0:T(8,128)(2,1)} fusion(f32[2,12,512,512]{2,3,1,0:T(8,128)} %get-tuple-element.87, f32[2,12,512]{2,1,0:T(8,128)S(1)} %get-tuple-element.86, f32[2,12,512]{2,1,0:T(8,128)S(1)} %log_add_fusion, f32[2,12,512,512]{2,3,1,0:T(8,128)} %get-tuple-element.78, pred[2,512,512]{1,2,0:T(8,128)(4,1)S(1)} %copy-done.3), kind=kLoop, calls=%fused_computation | loop fusion | flops 37748736 | bytes 63537152 | tf_op jit(solution)/shard_map/vmap()/convert_element_type | solution.py:79
  293.2 8.5 %multiply_bitcast_fusion = bf16[2,512,12,1,64]{1,4,2,0,3:T(8,128)(2,1)S(1)} fusion(bf16[2,12,512,512]{2,3,1,0:T(8,128)(2,1)} %multiply_convert_fusion, bf16[2,512,12,3,64]{1,4,2,0,3:T(8,128)(2,1)S(1)} %bitcast.134), kind=kOutput, calls=%fused_computation.42 | convolution fusion | flops 806879232 | bytes 15728640 | tf_op jit(solution)/shard_map/vmap(hqk,qhe->khe)/dot_general | solution.py:83
  301.7 6.8 %multiply_bitcast_fusion.1 = bf16[2,512,12,1,64]{1,4,2,0,3:T(8,128)(2,1)S(1)} fusion(bf16[2,12,512,512]{2,3,1,0:T(8,128)(2,1)} %multiply_convert_fusion, bf16[2,512,12,3,64]{1,4,2,0,3:T(8,128)(2,1)S(1)} %bitcast.134), kind=kOutput, calls=%fused_computation.43 | convolution fusion | flops 806879232 | bytes 15728640 | tf_op jit(solution)/shard_map/vmap(hqk,khe->qhe)/dot_general | solution.py:80
  308.5 2.6 convert_reduce_fusion
  311.1 0.1 reshape_squeeze.8
  311.3 0.1 reshape.254
  311.4 0.7 select_maximum_fusion.refs_4_
  312.2 9.4 %copy.72 = bf16[2,512,12,3,64]{1,0,4,3,2:T(2,128)(2,1)} copy(bf16[2,512,12,3,64]{1,4,2,0,3:T(8,128)(2,1)} %get-tuple-element.73) | data formatting | bytes 9437184 | tf_op jit(solution)/shard_map/vmap()/convert_element_type | solution.py:86
  321.5 9.1 %convert_element_type.114 = bf16[1024,4,576]{0,2,1:T(8,128)(2,1)} reshape(bf16[2,512,12,3,64]{1,0,4,3,2:T(2,128)(2,1)} %copy.72) | data formatting | bytes 9437184 | tf_op jit(solution)/shard_map/vmap()/convert_element_type | solution.py:86
  330.7 9.7 %bitcast_add_fusion = f32[1024,768]{1,0:T(8,128)} fusion(f32[1024,768]{1,0:T(8,128)S(1)} %copy-done.5, bf16[1024,4,576]{0,2,1:T(8,128)(2,1)} %convert_element_type.114, bf16[4,768,576]{2,1,0:T(8,128)(2,1)} %bitcast.157), kind=kOutput, calls=%fused_computation.28 | convolution fusion | flops 3624665088 | bytes 14548992 | tf_op jit(solution)/shard_map/tge,gde->td/dot_general | solution.py:645
  340.4 4.0 convert_bitcast_fusion
  344.4 3.9 copy.74
  348.4 108.1 %scatter_grads.1 = (f32[96,576]{1,0:T(8,128)}, f32[96,192]{1,0:T(8,128)}, f32[96,768]{1,0:T(8,128)}, f32[192,384]{1,0:T(8,128)}, f32[8,128]{1,0:T(8,128)}) custom-call(bf16[4,8,96,576]{3,2,1,0:T(8,128)(2,1)} %bitcast.135, bf16[4,8,96,192]{3,2,1,0:T(8,128)(2,1)} %bitcast.136, bf16[768,3072]{1,0:T(8,128)(2,1)} %convolution_convert_fusion.1.refs_2_, ...), custom_call_target="tpu_custom_call" | custom-call | tf_op jit(solution)/shard_map/scatter_grads/pallas_call | solution.py:537
  456.5 1.2 slice.79
  457.7 1.2 slice.78
  458.9 1.7 copy.106
  460.6 1.5 copy.107
  462.1 1.7 copy.108
  463.8 1.7 copy.109
  (96 shorter events, 1.3 us)
Async XLA Ops:
  3.6 143.8 %copy-start.2 = (pred[2,512,512]{1,2,0:T(8,128)(4,1)}, pred[2,512,512]{1,2,0:T(8,128)(4,1)S(1)}, u32[]{:S(2)}) copy-start(pred[2,512,512]{1,2,0:T(8,128)(4,1)S(1)} %compare_and_fusion) | copy-start | bytes 1572868
  90.6 5.5 %copy-start.12 = (bf16[4,8,96,192]{3,2,1,0:T(8,128)(2,1)S(1)}, bf16[4,8,96,192]{3,2,1,0:T(8,128)(2,1)}, u32[]{:S(2)}) copy-start(bf16[4,8,96,192]{3,2,1,0:T(8,128)(2,1)} %get-tuple-element.20) | copy-start | bytes 3538948
  125.8 21.6 %copy-start = (bf16[2,512,12,3,64]{1,4,2,0,3:T(8,128)(2,1)}, bf16[2,512,12,3,64]{1,4,2,0,3:T(8,128)(2,1)S(1)}, u32[]{:S(2)}) copy-start(bf16[2,512,12,3,64]{1,4,2,0,3:T(8,128)(2,1)S(1)} %fusion.11) | copy-start | bytes 14155780
  159.3 2.1 copy-start.16
  161.4 1.7 copy-start.10
  161.4 3.2 slice-start.2
  161.4 3.6 slice-start.3
  163.1 11.4 %copy-start.6 = (f32[1024,768]{1,0:T(8,128)}, f32[1024,768]{1,0:T(8,128)S(1)}, u32[]{:S(2)}) copy-start(f32[1024,768]{1,0:T(8,128)S(1)} %get-tuple-element.80) | copy-start | bytes 9437188
  163.1 11.3 %slice-start.6 = ((s8[4718592]{0:T(1024)(128)(4,1)}), s8[4194304]{0:T(1024)(128)(4,1)S(1)}, s32[]{:S(2)}) async-start(s8[4718592]{0:T(1024)(128)(4,1)} %bitcast.154), calls=%async_computation.6 | async-start | bytes 8388608
  165.1 9.4 %slice-start.7 = ((s8[4718592]{0:T(1024)(128)(4,1)}), s8[524288]{0:T(1024)(128)(4,1)S(1)}, s32[]{:S(2)}) async-start(s8[4718592]{0:T(1024)(128)(4,1)} %bitcast.154), calls=%async_computation.7 | async-start | bytes 1048576
  174.4 5.5 %copy-start.20 = (bf16[1024,3072]{1,0:T(8,128)(2,1)}, bf16[1024,3072]{1,0:T(8,128)(2,1)S(1)}, u32[]{:S(2)}) copy-start(bf16[1024,3072]{1,0:T(8,128)(2,1)S(1)} %get-tuple-element.81) | copy-start | bytes 18874372
  179.9 1.4 copy-start.1
  182.6 15.6 %slice-start.8 = ((s8[6291456]{0:T(1024)(128)(4,1)}), s8[4194304]{0:T(1024)(128)(4,1)S(1)}, s32[]{:S(2)}) async-start(s8[6291456]{0:T(1024)(128)(4,1)} %bitcast.162), calls=%async_computation.8 | async-start | bytes 8388608
  182.6 22.9 %slice-start.4 = ((s8[4718592]{0:T(1024)(128)(4,1)}), s8[4194304]{0:T(1024)(128)(4,1)S(1)}, s32[]{:S(2)}) async-start(s8[4718592]{0:T(1024)(128)(4,1)} %bitcast.152), calls=%async_computation.4 | async-start | bytes 8388608
  186.2 12.0 %slice-start.9 = ((s8[6291456]{0:T(1024)(128)(4,1)}), s8[2097152]{0:T(1024)(128)(4,1)S(1)}, s32[]{:S(2)}) async-start(s8[6291456]{0:T(1024)(128)(4,1)} %bitcast.162), calls=%async_computation.9 | async-start | bytes 4194304
  186.2 19.4 %slice-start.5 = ((s8[4718592]{0:T(1024)(128)(4,1)}), s8[524288]{0:T(1024)(128)(4,1)S(1)}, s32[]{:S(2)}) async-start(s8[4718592]{0:T(1024)(128)(4,1)} %bitcast.152), calls=%async_computation.5 | async-start | bytes 1048576
  198.2 7.3 %copy-start.18 = (bf16[1024,3072]{1,0:T(8,128)(2,1)}, bf16[1024,3072]{1,0:T(8,128)(2,1)S(1)}, u32[]{:S(2)}) copy-start(bf16[1024,3072]{1,0:T(8,128)(2,1)S(1)} %get-tuple-element.89) | copy-start | bytes 18874372
  198.3 7.3 %copy-start.7 = (f32[1024,768]{1,0:T(8,128)S(1)}, f32[1024,768]{1,0:T(8,128)}, u32[]{:S(2)}) copy-start(f32[1024,768]{1,0:T(8,128)} %copy-done.6) | copy-start | bytes 9437188
  213.3 3.8 copy-start.8
  213.3 5.6 %copy-start.19 = (bf16[1024,3072]{1,0:T(8,128)(2,1)S(1)}, bf16[1024,3072]{1,0:T(8,128)(2,1)}, u32[]{:S(2)}) copy-start(bf16[1024,3072]{1,0:T(8,128)(2,1)} %copy-done.18) | copy-start | bytes 18874372
  218.9 7.9 %copy-start.4 = (f32[1024,768]{1,0:T(8,128)}, f32[1024,768]{1,0:T(8,128)S(1)}, u32[]{:S(2)}) copy-start(f32[1024,768]{1,0:T(8,128)S(1)} %get-tuple-element.71) | copy-start | bytes 9437188
  228.1 2.0 copy-start.11
  230.1 2.5 copy-start.13
  236.2 5.5 %copy-start.3 = (pred[2,512,512]{1,2,0:T(8,128)(4,1)S(1)}, pred[2,512,512]{1,2,0:T(8,128)(4,1)}, u32[]{:S(2)}) copy-start(pred[2,512,512]{1,2,0:T(8,128)(4,1)} %copy-done.2) | copy-start | bytes 1572868
  254.3 38.9 %slice-start = ((s8[4718592]{0:T(1024)(128)(4,1)}), s8[524288]{0:T(1024)(128)(4,1)S(1)}, s32[]{:S(2)}) async-start(s8[4718592]{0:T(1024)(128)(4,1)} %bitcast.133), calls=%async_computation | async-start | bytes 1048576
  271.5 21.7 %slice-start.1 = ((s8[4718592]{0:T(1024)(128)(4,1)}), s8[4194304]{0:T(1024)(128)(4,1)S(1)}, s32[]{:S(2)}) async-start(s8[4718592]{0:T(1024)(128)(4,1)} %bitcast.133), calls=%async_computation.1 | async-start | bytes 8388608
  301.7 6.8 %copy-start.14 = (bf16[2,512,12,1,64]{1,4,2,0,3:T(8,128)(2,1)S(1)}, bf16[2,512,12,1,64]{1,4,2,0,3:T(8,128)(2,1)}, u32[]{:S(2)}) copy-start(bf16[2,512,12,1,64]{1,4,2,0,3:T(8,128)(2,1)} %fusion.24) | copy-start | bytes 4718596
  308.5 2.9 copy-start.15
  321.5 9.2 %copy-start.5 = (f32[1024,768]{1,0:T(8,128)S(1)}, f32[1024,768]{1,0:T(8,128)}, u32[]{:S(2)}) copy-start(f32[1024,768]{1,0:T(8,128)} %copy-done.4) | copy-start | bytes 9437188
  330.7 9.7 %copy-start.9 = (bf16[1024,4,576]{0,2,1:T(8,128)(2,1)S(1)}, bf16[1024,4,576]{0,2,1:T(8,128)(2,1)}, u32[]{:S(2)}) copy-start(bf16[1024,4,576]{0,2,1:T(8,128)(2,1)} %convert_element_type.114) | copy-start | bytes 14155780
  330.7 9.7 %copy-start.17 = (bf16[2,1,512,768]{3,2,1,0:T(8,128)(2,1)S(1)}, bf16[2,1,512,768]{3,2,1,0:T(8,128)(2,1)}, u32[]{:S(2)}) copy-start(bf16[2,1,512,768]{3,2,1,0:T(8,128)(2,1)} %param.10) | copy-start | bytes 4718596
